TPU v7x, 32 devices: a whole 2x2x4 slice. The times are simulated.
32 devices in a mesh: gz: 32 (over z, y, x, core).
Axes of the slice: x: 2, y: 2, z: 4, core: 2. Of those that a mesh axis runs over, the one named last changes fastest.
Arguments:
- density: float32 [2, 32, 256, 256], P(None, 'gz'), may hold values from 0.02 to 0.8
- kernel_hat: float32 [64, 512, 512], P(None, 'gz'), may hold values from 0.37 to 7, as said below
Outputs:
- potential: float32 [2, 32, 256, 256], P(None, 'gz')
- energies: float32 [2], replicated
Inputs may be any that keep to these rules, and one draw needn't show every extreme that they name: kernel_hat at (a, b, c) equals kernel_hat at ((-a) mod 64, (-b) mod 512, (-c) mod 512).
All inputs are finite; a program needn't handle non-finite values.
Results may differ from a plain program's by a relative error of at most 0.00015.
Values sent between devices are 32-bit elements; how exact they have to be, the bound alone decides.
A program may use at most 64 MiB of HBM per device.

v0:
```python
import functools
import math

import jax
import jax.numpy as jnp
import numpy as np
from jax import lax
from jax.experimental import pallas as pl
from jax.experimental.pallas import tpu as pltpu
from jax.sharding import PartitionSpec as P

HGRID = 0.35
STENCIL = (0.8, -0.2, 4.0 / 105.0, -1.0 / 280.0)
KAPPA = 0.804
MU_X = 0.2195149727645171
BETA_C = 0.06672455060314922
GAMMA_C = 0.031090690869654894
FZ_CURV = 1.709921
PARAMS_UNPOL = (0.031091, 0.2137, 7.5957, 3.5876, 1.6382, 0.49294)
PARAMS_POL = (0.015545, 0.20548, 14.1189, 6.1977, 3.3662, 0.62517)
PARAMS_STIFF = (0.016887, 0.11125, 10.357, 3.6231, 0.88026, 0.49671)


def shifted(value, axis, steps):
    count = lax.axis_size(axis)
    leading, last = (max(0, -steps), min(count, count - steps))
    return lax.ppermute(value, axis, [(source, source + steps) for source in range(leading, last)])


def inner_slope(extended, direction):
    stencil_reach = len(STENCIL)
    length_out = extended.shape[direction] - 2 * stencil_reach
    result = 0.0
    for offset, weight in enumerate(STENCIL):
        upper_part = lax.slice_in_dim(
            extended,
            stencil_reach + offset + 1,
            stencil_reach + offset + 1 + length_out,
            axis=direction,
        )
        lower_part = lax.slice_in_dim(
            extended,
            stencil_reach - offset - 1,
            stencil_reach - offset - 1 + length_out,
            axis=direction,
        )
        result = result + weight * (upper_part - lower_part)
    return result / HGRID


def plane_slope(field, direction):
    stencil_reach = len(STENCIL)
    widths = [(0, 0)] * field.ndim
    widths[direction] = (stencil_reach, stencil_reach)
    return inner_slope(jnp.pad(field, widths), direction)


def pw_piece(radius, params):
    half_root = jnp.sqrt(radius)
    series = (
        params[2] * half_root
        + params[3] * radius
        + params[4] * radius * half_root
        + params[5] * radius * radius
    )
    return (
        -2.0 * params[0] * (1.0 + params[1] * radius) * jnp.log1p(1.0 / (2.0 * params[0] * series))
    )


def exchange_part(doubled, cube_root, sigma_four):
    uniform_part = -0.75 * (3.0 / math.pi) ** (1.0 / 3.0) * cube_root
    reduced = sigma_four / (4.0 * (3.0 * math.pi**2) ** (2.0 / 3.0) * doubled**2 * cube_root**2)
    enhance = 1.0 + KAPPA - KAPPA / (1.0 + MU_X * reduced / KAPPA)
    return doubled * uniform_part * enhance


def energy_density(dens_up, dens_down, sigma_uu, sigma_ud, sigma_dd):
    up_cube = jnp.cbrt(2.0 * dens_up)
    down_cube = jnp.cbrt(2.0 * dens_down)
    exchange_term = 0.5 * exchange_part(
        2.0 * dens_up, up_cube, 4.0 * sigma_uu
    ) + 0.5 * exchange_part(2.0 * dens_down, down_cube, 4.0 * sigma_dd)
    density_sum = dens_up + dens_down
    sum_cube = jnp.cbrt(density_sum)
    polarization = (dens_up - dens_down) / density_sum
    radius = (3.0 / (4.0 * math.pi)) ** (1.0 / 3.0) / sum_cube
    plus_side = 1.0 + polarization
    minus_side = 1.0 - polarization
    plus_cube = up_cube / sum_cube
    minus_cube = down_cube / sum_cube
    spin_weight = (plus_side * plus_cube + minus_side * minus_cube - 2.0) / (
        2.0 ** (4.0 / 3.0) - 2.0
    )
    unpolar = pw_piece(radius, PARAMS_UNPOL)
    polarized = pw_piece(radius, PARAMS_POL)
    stiffness = pw_piece(radius, PARAMS_STIFF)
    polar_four = polarization**4
    local_corr = (
        unpolar
        - stiffness * spin_weight * (1.0 - polar_four) / FZ_CURV
        + (polarized - unpolar) * spin_weight * polar_four
    )
    phi_factor = 0.5 * (plus_cube**2 + minus_cube**2)
    phi_cubed = phi_factor**3
    screening_sq = 4.0 * (3.0 * math.pi**2) ** (1.0 / 3.0) / math.pi * sum_cube
    sigma_total = sigma_uu + 2.0 * sigma_ud + sigma_dd
    scaled_sq = sigma_total / (4.0 * phi_factor**2 * screening_sq * density_sum**2)
    weight_a = BETA_C / GAMMA_C / jnp.expm1(-local_corr / (GAMMA_C * phi_cubed))
    gradient_term = (
        GAMMA_C
        * phi_cubed
        * jnp.log1p(
            BETA_C
            / GAMMA_C
            * scaled_sq
            * (1.0 + weight_a * scaled_sq)
            / (1.0 + weight_a * scaled_sq + weight_a**2 * scaled_sq**2)
        )
    )
    return exchange_term + density_sum * (local_corr + gradient_term)


def flux_pair(deriv_uu, deriv_ud, deriv_dd, gradient):
    return jnp.stack(
        [
            2.0 * deriv_uu * gradient[0] + deriv_ud * gradient[1],
            2.0 * deriv_dd * gradient[1] + deriv_ud * gradient[0],
        ]
    )


def xc_fields(dens, grad_z, grad_y, grad_x):
    sigma_uu = grad_z[0] * grad_z[0] + grad_y[0] * grad_y[0] + grad_x[0] * grad_x[0]
    sigma_ud = grad_z[0] * grad_z[1] + grad_y[0] * grad_y[1] + grad_x[0] * grad_x[1]
    sigma_dd = grad_z[1] * grad_z[1] + grad_y[1] * grad_y[1] + grad_x[1] * grad_x[1]
    energy, pullback = jax.vjp(energy_density, dens[0], dens[1], sigma_uu, sigma_ud, sigma_dd)
    d_up, d_down, d_uu, d_ud, d_dd = pullback(jnp.ones_like(energy))
    return (
        energy,
        jnp.stack([d_up, d_down]),
        flux_pair(d_uu, d_ud, d_dd, grad_z),
        flux_pair(d_uu, d_ud, d_dd, grad_y),
        flux_pair(d_uu, d_ud, d_dd, grad_x),
    )


MESH = pl.DeviceIdType.MESH
LANES = 128
SUBLANES = 8
VMEM_SPEC = pl.BlockSpec(memory_space=pltpu.VMEM)
VMEM_BYTES = 60 * 1024 * 1024


def extend_rows(field, depth):
    rows = field.shape[2]
    below_parts = []
    above_parts = []
    for distance in range(1, -(-depth // rows) + 1):
        needed = min(rows, depth - (distance - 1) * rows)
        below_parts.insert(0, shifted(field[:, :, rows - needed :], "gz", distance))
        above_parts.append(shifted(field[:, :, :needed], "gz", -distance))
    return jnp.concatenate(below_parts + [field] + above_parts, axis=2)


def split(value):
    high = value.astype(jnp.bfloat16)
    low = (value - high.astype(jnp.float32)).astype(jnp.bfloat16)
    return high, low


def np_split(table):
    table = np.asarray(table, np.float32)
    high = table.astype(jnp.bfloat16)
    low = (table - high.astype(np.float32)).astype(jnp.bfloat16)
    return high, low


def angles(spatial, spectral):
    index = np.outer(np.arange(spatial), np.arange(spectral)) % spectral
    return index * (2.0 * np.pi / spectral)


def y_tables(width_y, devices, scale):
    angle = angles(width_y, 2 * width_y)
    both = np.stack([np.cos(angle), -np.sin(angle)])
    both = both.reshape(2, width_y, devices, -1).transpose(2, 0, 3, 1)
    forward = both.reshape(4 * width_y, width_y)
    return np_split(forward), np_split(forward.T * scale)


def x_table(width_x):
    angle = angles(width_x, 2 * width_x)[:, :width_x]
    sine = np.sin(angle)
    sine[:, 0] = (-1.0) ** np.arange(width_x)
    return np_split(np.concatenate([np.cos(angle), sine], axis=1))


def z_tables(depth_z):
    angle = angles(depth_z, 2 * depth_z)
    cos, sin = np.cos(angle).T, np.sin(angle).T
    forward = np.block([[cos, sin], [-sin, cos]])
    out = []
    for table in (forward, forward.T):
        high, low = np_split(table)
        out.append(np.concatenate([high, high, low], axis=1))
    return out


def dot(left, right):
    return jnp.dot(left, right, preferred_element_type=jnp.float32)


def stacked(value):
    high, low = split(value)
    return jnp.concatenate([high, low, high], axis=0)


def greet(devices):
    me = lax.axis_index("gz")
    barrier = pltpu.get_barrier_semaphore()

    def signal(step, carry):
        pl.semaphore_signal(
            barrier,
            inc=1,
            device_id=(lax.rem(me + step, devices),),
            device_id_type=MESH,
        )
        return carry

    lax.fori_loop(1, devices, signal, 0)
    return lambda: pl.semaphore_wait(barrier, devices - 1)


def remote(devices, pieces, sends, receives):
    me = lax.axis_index("gz")

    def each(step, source_of, slot_of, act):
        for piece, (source, target) in enumerate(pieces):
            act(
                pltpu.make_async_remote_copy(
                    src_ref=source(source_of),
                    dst_ref=target(slot_of),
                    send_sem=sends.at[piece, step],
                    recv_sem=receives.at[piece, step],
                    device_id=(source_of,),
                    device_id_type=MESH,
                )
            )

    def start(step, carry):
        each(step, lax.rem(me + step, devices), me, lambda copy: copy.start())
        return carry

    def finish(step, carry):
        peer = lax.rem(me + step, devices)
        origin = lax.rem(me - step + devices, devices)
        each(step, peer, me, lambda copy: copy.wait_send())
        each(step, peer, origin, lambda copy: copy.wait_recv())
        return carry

    lax.fori_loop(1, devices, start, 0)
    return lambda: lax.fori_loop(1, devices, finish, 0)


def forward_kernel(devices, dens, t_high, t_low, dens_out, spec_out, spec, sends, receives):
    me = lax.axis_index("gz")
    arrived = greet(devices)
    width_y = t_high.shape[1]
    total = (dens[0] + dens[1]).reshape(width_y, dens.shape[3])
    high, low = split(total)
    values = dot(t_high[...], high) + (dot(t_high[...], low) + dot(t_low[...], high))
    spec[...] = values.reshape(spec.shape)
    arrived()
    finish = remote(
        devices,
        [
            (lambda peer: dens.at[:, peer], lambda slot: dens_out.at[:, slot]),
            (lambda peer: spec.at[peer], lambda slot: spec_out.at[slot]),
        ],
        sends,
        receives,
    )
    dens_out[:, me] = dens[:, me]
    spec_out[me] = spec[me]
    finish()


def forward_exchange(devices, dens, tables):
    width_x = dens.shape[3]
    spec_shape = (devices, tables[0].shape[0] // devices, width_x)
    return pl.pallas_call(
        functools.partial(forward_kernel, devices),
        out_shape=(
            jax.ShapeDtypeStruct(dens.shape, jnp.float32),
            jax.ShapeDtypeStruct(spec_shape, jnp.float32),
        ),
        in_specs=[VMEM_SPEC] * 3,
        out_specs=(VMEM_SPEC, VMEM_SPEC),
        scratch_shapes=[
            pltpu.VMEM(spec_shape, jnp.float32),
            pltpu.SemaphoreType.DMA((2, devices)),
            pltpu.SemaphoreType.DMA((2, devices)),
        ],
        compiler_params=pltpu.CompilerParams(
            collective_id=0, has_side_effects=True, vmem_limit_bytes=VMEM_BYTES
        ),
        name="forward_exchange",
    )(dens, *tables)


def filter_kernel(spec, kernel_hat, edge, tx_high, tx_low, z_fore, z_back, out, energy, held, wide):
    depth, rows, width = spec.shape
    count = rows // 2
    for q in range(count):
        held[q, :depth] = spec[:, q, :]
        held[q, depth:] = spec[:, count + q, :]

    def times_x(value):
        high, low = split(value.reshape(count * 2 * depth, width))
        result = dot(high, tx_high[...]) + (dot(low, tx_high[...]) + dot(high, tx_low[...]))
        wide[...] = result.reshape(wide.shape)

    lane = lax.broadcasted_iota(jnp.int32, (1, width), 1)
    first = lane == 0
    weight = jnp.where(first, 1.0, 2.0)
    alternate = jnp.where(lane % 2 == 0, 1.0, -1.0)
    edge_lane = lax.broadcasted_iota(jnp.int32, (1, LANES), 1)
    times_x(held[...])
    last = jnp.zeros((2 * depth, LANES), jnp.float32)
    edge_factor = jnp.zeros((2 * depth, LANES), jnp.float32)
    for q in range(count):
        cos_part = wide[q, :, :width]
        sin_part = wide[q, :, width:]
        last = jnp.where(edge_lane == q, sin_part[:, :1], last)
        edge_factor = jnp.where(edge_lane == q, edge[:, q, :1], edge_factor)
        sin_part = jnp.where(first, 0.0, sin_part)
        value = jnp.concatenate(
            [cos_part[:depth] + sin_part[depth:], cos_part[depth:] - sin_part[:depth]], axis=0
        )
        value = dot(z_fore[...], stacked(value))
        factor = kernel_hat[:, q, :] * weight
        value = value * jnp.concatenate([factor, factor], axis=0)
        wide[q, :, :width] = dot(z_back[...], stacked(value))
    last = dot(z_fore[...], stacked(last))
    last = last * jnp.concatenate([edge_factor, edge_factor], axis=0)
    last = dot(z_back[...], stacked(last))
    times_x(wide[:, :, :width])
    acc = jnp.zeros((depth, width), jnp.float32)
    for q in range(count):
        cos_part = wide[q, :, :width] + last[:, q : q + 1] * alternate
        sin_part = jnp.where(first, 0.0, wide[q, :, width:])
        real = cos_part[:depth] - sin_part[depth:]
        imag = cos_part[depth:] + sin_part[:depth]
        acc = acc + (held[q, :depth] * real + held[q, depth:] * imag)
        out[:, q, :] = real
        out[:, count + q, :] = imag
    energy[...] = jnp.full(energy.shape, jnp.sum(acc))


def filtered(spec, kernel_hat):
    depth, rows, width = spec.shape
    count = rows // 2
    tables = (*x_table(width), *z_tables(depth))
    whole = [pl.BlockSpec(array.shape, lambda i, r=array.ndim: (0,) * r) for array in tables]
    return pl.pallas_call(
        filter_kernel,
        grid=(1,),
        out_shape=(
            jax.ShapeDtypeStruct(spec.shape, jnp.float32),
            jax.ShapeDtypeStruct((SUBLANES, LANES), jnp.float32),
        ),
        in_specs=[
            pl.BlockSpec(spec.shape, lambda i: (0, 0, 0)),
            pl.BlockSpec((2 * depth, count, width), lambda i: (0, 0, 0)),
            pl.BlockSpec((2 * depth, count, LANES), lambda i: (0, 0, width // LANES)),
            *whole,
        ],
        out_specs=(
            pl.BlockSpec(spec.shape, lambda i: (0, 0, 0)),
            pl.BlockSpec((SUBLANES, LANES), lambda i: (0, 0)),
        ),
        scratch_shapes=[
            pltpu.VMEM((count, 2 * depth, width), jnp.float32),
            pltpu.VMEM((count, 2 * depth, 2 * width), jnp.float32),
        ],
        compiler_params=pltpu.CompilerParams(vmem_limit_bytes=VMEM_BYTES),
        cost_estimate=pl.CostEstimate(
            flops=10**10, bytes_accessed=4 * 10**6, transcendentals=0
        ),
        name="kernel_filter",
    )(spec, kernel_hat, kernel_hat, *tables)


def backward_kernel(
    devices, spec, v_rows, partial, t_high, t_low, out, e_out, v_all, sums, sends, receives
):
    me = lax.axis_index("gz")
    greet(devices)()
    finish = remote(
        devices,
        [
            (lambda peer: v_rows.at[:, peer], lambda slot: v_all.at[:, slot]),
            (lambda peer: partial, lambda slot: sums.at[slot]),
        ],
        sends,
        receives,
    )
    v_all[:, me] = v_rows[:, me]
    sums[me] = partial[...]
    high, low = split(spec[...].reshape(t_high.shape[1], spec.shape[2]))
    values = dot(t_high[...], high) + (dot(t_high[...], low) + dot(t_low[...], high))
    out[0] = values.reshape(out.shape[1:])
    finish()
    e_out[...] = jnp.sum(sums[...], axis=0)
    values = out[0]
    out[0] = values + v_all[0]
    out[1] = values + v_all[1]


def backward_exchange(devices, spec, v_rows, partial, tables):
    return pl.pallas_call(
        functools.partial(backward_kernel, devices),
        out_shape=(
            jax.ShapeDtypeStruct(v_rows.shape, jnp.float32),
            jax.ShapeDtypeStruct(partial.shape, jnp.float32),
        ),
        in_specs=[VMEM_SPEC] * 5,
        out_specs=(VMEM_SPEC,) * 2,
        scratch_shapes=[
            pltpu.VMEM(v_rows.shape, jnp.float32),
            pltpu.VMEM((devices, *partial.shape), jnp.float32),
            pltpu.SemaphoreType.DMA((2, devices)),
            pltpu.SemaphoreType.DMA((2, devices)),
        ],
        compiler_params=pltpu.CompilerParams(
            collective_id=1, has_side_effects=True, vmem_limit_bytes=VMEM_BYTES
        ),
        name="backward_exchange",
    )(spec, v_rows, partial, *tables)


def xc_rows(dens, extended):
    stencil_reach = len(STENCIL)
    grad_z = plane_slope(dens, 1)
    grad_x = plane_slope(dens, 3)
    grad_y = inner_slope(extended, 2)
    energy, d_dens, flux_z, flux_y, flux_x = xc_fields(dens, grad_z, grad_y, grad_x)
    divergence_y = inner_slope(extend_rows(flux_y, stencil_reach), 2)
    v_xc = d_dens - (plane_slope(flux_z, 1) + divergence_y + plane_slope(flux_x, 3))
    return v_xc, jnp.sum(energy)


def per_device(density, kernel_hat):
    planes, width_y, width_x = density.shape[1:]
    devices = lax.axis_size("gz")
    assert planes == 1
    depth_z = planes * devices
    cell_count = depth_z * width_y * width_x
    forward, inverse = y_tables(width_y, devices, 1.0 / (8 * cell_count))
    dens, spec = forward_exchange(
        devices, density.reshape(2, devices, width_y // devices, width_x), forward
    )
    extended = extend_rows(dens, len(STENCIL))
    back, energy_h = filtered(spec, kernel_hat)
    dens, extended, back = lax.optimization_barrier((dens, extended, back))
    back = lax.all_to_all(back, "gz", split_axis=0, concat_axis=0, tiled=True)
    v_rows, energy_xc = xc_rows(dens, extended)
    row = lax.broadcasted_iota(jnp.int32, energy_h.shape, 0)
    partial = jnp.where(
        row == 0, energy_xc / cell_count, energy_h * (0.5 / (8.0 * cell_count) / cell_count)
    )
    potential, sums = backward_exchange(devices, back, v_rows, partial, inverse)
    return (potential.reshape(density.shape), sums[:2, 0])


def solution(mesh):
    placed = (P(None, "gz", None, None), P(None, "gz", None))
    return jax.shard_map(
        per_device,
        mesh=mesh,
        in_specs=placed,
        out_specs=(P(None, "gz", None, None), P()),
        check_vma=False,
    )
```

profile of v0, /device:TPU:15, one launch (start us, length us, event | category | flops | bytes accessed | tf_op | source)
XLA Modules:
  0.0 123.3 jit_solution(14481604993129081860)
XLA Ops:
  0.6 45.5 %forward_exchange.1 = (f32[2,32,8,256]{3,2,1,0:T(8,128)}, f32[32,32,256]{2,1,0:T(8,128)}) custom-call(f32[2,32,8,256]{3,2,1,0:T(8,128)} %bitcast.105, bf16[1024,256]{1,0:T(8,128)(2,1)} %constant.162.clone.t_high, bf16[1024,256]{1,0:T(8,128)(2,1)} %constant.163.clone.t_low), custom_call_target="tpu_custom_call" | custom-call | tf_op jit(solution)/shard_map/forward_exchange/pallas_call | solution.py:293
  46.2 1.3 %fusion.169 = (f32[2,32,4,256]{3,2,1,0:T(4,128)S(1)}, f32[2,32,4,256]{3,2,1,0:T(4,128)S(1)}) fusion(f32[2,32,8,256]{3,2,1,0:T(8,128)} %get-tuple-element.15), kind=kLoop, calls=%fused_computation.303 | loop fusion | bytes 1048576 | tf_op jit(solution)/shard_map/slice | solution.py:161
  47.5 1.9 %collective-permute-start = (f32[2,32,4,256]{3,2,1,0:T(4,128)S(1)}, f32[2,32,4,256]{3,2,1,0:T(4,128)S(1)}, u32[]{:S(2)}, u32[]{:S(2)}) collective-permute-start(f32[2,32,4,256]{3,2,1,0:T(4,128)S(1)} %get-tuple-element.55), channel_id=1, source_target_pairs={{0,1},{1,2},{2,3},{3,4},{4,5},{5,6},{6,7},{7,8},{8,9},{9,10},{10,1... | collective-permute-start | bytes 786440 | tf_op jit(solution)/shard_map/ppermute | solution.py:27
  49.4 2.4 %collective-permute-start.1 = (f32[2,32,4,256]{3,2,1,0:T(4,128)S(1)}, f32[2,32,4,256]{3,2,1,0:T(4,128)S(1)}, u32[]{:S(2)}, u32[]{:S(2)}) collective-permute-start(f32[2,32,4,256]{3,2,1,0:T(4,128)S(1)} %get-tuple-element.56), channel_id=1, source_target_pairs={{1,0},{2,1},{3,2},{4,3},{5,4},{6,5},{7,6},{8,7},{9,8},{10,9},{11,1... | collective-permute-start | bytes 786440 | tf_op jit(solution)/shard_map/ppermute | solution.py:27
  51.8 0.0 copy-start
  51.8 7.3 %kernel_filter.1 = (f32[32,32,256]{2,1,0:T(8,128)}, f32[8,128]{1,0:T(8,128)}) custom-call(f32[32,32,256]{2,1,0:T(8,128)} %get-tuple-element.12.spec, f32[64,16,512]{2,1,0:T(8,128)} %edge.1, f32[64,16,512]{2,1,0:T(8,128)} %edge.1, bf16[256,512]{1,0:T(8,128)(2,1)} %constant.164.clone.tx_high, bf16[256,512]{1,0:T(8,128)(2,1)} %constant.165.clone.tx_low, ...), custom_call_target="tpu_custom_call" | custom-call | flops 10000000000 | bytes 4000000 | tf_op jit(solution)/shard_map/kernel_filter/pallas_call | solution.py:367
  59.1 0.0 collective-permute-done
  59.1 0.0 collective-permute-done.1
  59.2 0.0 copy-done
  59.2 0.2 pad_maximum_fusion
  59.4 5.8 %all-to-all-start = ((f32[32,32,256]{2,1,0:T(8,128)}), f32[32,32,256]{2,1,0:T(8,128)S(1)}, u32[]{:S(2)}, u32[]{:S(2)}) async-start(f32[32,32,256]{2,1,0:T(8,128)} %get-tuple-element.14), calls=%async_computation | async-start | bytes 2097152 | tf_op jit(solution)/shard_map/all_to_all | solution.py:468
  65.2 1.5 %fusion.152 = (f32[1,32,8,256]{3,2,1,0:T(8,128)S(1)}, f32[1,32,8,256]{3,2,1,0:T(8,128)S(1)}) fusion(f32[2,32,8,256]{3,2,1,0:T(8,128)S(1)} %copy-done), kind=kLoop, calls=%fused_computation.269 | loop fusion | flops 4718592 | bytes 1048576 | tf_op jit(solution)/shard_map/jvp()/neg | solution.py:109
  66.7 1.7 %fusion.19 = (f32[2,32,8,256]{3,2,1,0:T(8,128)S(1)}, f32[2,32,8,256]{3,2,1,0:T(8,128)S(1)}, f32[2,32,8,256]{3,2,1,0:T(8,128)S(1)}) fusion(f32[2,32,8,256]{3,2,1,0:T(8,128)S(1)} %copy-done, f32[2,32,16,256]{3,2,1,0:T(8,128)S(1)} %pad_maximum_fusion), kind=kLoop, calls=%fused_computation.44 | loop fusion | flops 4718592 | bytes 6291456 | tf_op jit(solution)/shard_map/div | solution.py:48
  68.4 3.0 %fusion.115 = (f32[]{:T(128)}, f32[1,32,8,256]{3,2,1,0:T(8,128)S(1)}, f32[1,32,8,256]{3,2,1,0:T(8,128)S(1)}, f32[1,32,8,256]{3,2,1,0:T(8,128)S(1)}) fusion(f32[2,32,8,256]{3,2,1,0:T(8,128)S(1)} %copy-done, f32[2,32,8,256]{3,2,1,0:T(8,128)S(1)} %get-tuple-element.53, f32[2,32,8,256]{3,2,1,0:T(8,128)S(1)} %get-tuple-element.57, ...), kind=kLoop, calls=%fused_computation.176 | loop fusion | flops 9633791 | bytes 2883588 | tf_op jit(solution)/shard_map/reduce_sum | solution.py:452
  71.5 4.4 %multiply_add_fusion.8 = (f32[1,32,8,256]{3,2,1,0:T(8,128)S(1)}, f32[1,32,8,256]{3,2,1,0:T(8,128)S(1)}, f32[1,32,8,256]{3,2,1,0:T(8,128)S(1)}, f32[1,32,8,256]{3...) fusion(f32[1,32,8,256]{3,2,1,0:T(8,128)S(1)} %get-tuple-element, ...), kind=kLoop, calls=%fused_computation.224 | loop fusion | flops 22282240 | bytes 3407872 | tf_op jit(solution)/shard_map/transpose(jvp())/add_any | solution.py:79
  75.8 0.5 multiply_add_fusion.5
  76.3 2.2 %multiply_add_fusion.4 = (f32[1,32,8,256]{3,2,1,0:T(8,128)S(1)}, f32[1,32,8,256]{3,2,1,0:T(8,128)S(1)}, f32[1,32,8,256]{3,2,1,0:T(8,128)S(1)}) fusion(f32[2,32,8,256]{3,2,1,0:T(8,128)S(1)} %get-tuple-element.54, f32[1,32,8,256]{3,2,1,0:T(8,128)S(1)} %get-tuple-element.37, f32[1,32,8,256]{3,2,1,0:T(8,128)S(1)} %get-tuple-element.27, ...), kind=kLoop, calls=%fused_computation.215 | loop fusion | flops 10092544 | bytes 3670016 | tf_op jit(solution)/shard_map/add | solution.py:128
  78.5 0.1 multiply_add_fusion.1
  78.6 0.0 copy-start.2
  78.6 0.9 fusion.113
  79.5 2.3 %collective-permute-start.2 = (f32[2,32,4,256]{3,2,1,0:T(4,128)}, f32[2,32,4,256]{3,2,1,0:T(4,128)}, u32[]{:S(2)}, u32[]{:S(2)}) collective-permute-start(f32[2,32,4,256]{3,2,1,0:T(4,128)} %get-tuple-element.51), channel_id=1, source_target_pairs={{1,0},{2,1},{3,2},{4,3},{5,4},{6,5},{7,6},{8,7},{9,8},{10,9},{11,1... | collective-permute-start | bytes 786440 | tf_op jit(solution)/shard_map/ppermute | solution.py:27
  81.8 5.3 %collective-permute-start.3 = (f32[2,32,4,256]{3,2,1,0:T(4,128)}, f32[2,32,4,256]{3,2,1,0:T(4,128)}, u32[]{:S(2)}, u32[]{:S(2)}) collective-permute-start(f32[2,32,4,256]{3,2,1,0:T(4,128)} %get-tuple-element.52), channel_id=1, source_target_pairs={{0,1},{1,2},{2,3},{3,4},{4,5},{5,6},{6,7},{7,8},{8,9},{9,10},{10,1... | collective-permute-start | bytes 786440 | tf_op jit(solution)/shard_map/ppermute | solution.py:27
  87.1 0.3 select_maximum_fusion
  88.1 0.0 copy-done.2
  88.1 0.7 multiply_select_fusion.partial
  88.8 4.1 %collective-permute-done.2 = f32[2,32,4,256]{3,2,1,0:T(4,128)} collective-permute-done((f32[2,32,4,256]{3,2,1,0:T(4,128)}, f32[2,32,4,256]{3,2,1,0:T(4,128)}, u32[]{:S(2)}, u32[]{:S(2)}) %collective-permute-start.2) | collective-permute-done | bytes 262176 | tf_op jit(solution)/shard_map/ppermute | solution.py:27
  92.9 0.0 collective-permute-done.3
  92.9 1.3 %pad_maximum_fusion.1 = (f32[2,32,12,256]{3,2,1,0:T(8,128)S(1)}, f32[2,32,12,256]{3,2,1,0:T(8,128)S(1)}) fusion(f32[2,32,4,256]{3,2,1,0:T(4,128)} %collective-permute-done.2, f32[1,32,8,256]{3,2,1,0:T(8,128)S(1)} %get-tuple-element.47, f32[1,32,8,256]{3,2,1,0:T(8,128)S(1)} %get-tuple-element.48, f32[2,32,4,256]{3,2,1,0:T(4,128)} %collective-permute-done.3), kind=kLoop, calls=%fused_computation.11 | loop fusion | flops 786432 | bytes 2621440 | tf_op jit(solution)/shard_map/concatenate | solution.py:163
  94.2 1.8 %fusion.30.v_rows = f32[2,32,8,256]{3,2,1,0:T(8,128)} fusion(f32[2,32,8,264]{3,2,1,0:T(8,128)S(1)} %select_maximum_fusion, f32[2,32,12,256]{3,2,1,0:T(8,128)S(1)} %get-tuple-element.50, f32[2,32,12,256]{3,2,1,0:T(8,128)S(1)} %get-tuple-element.49, f32[2,40,8,256]{3,2,1,0:T(8,128)S(1)} %select_maximum_fusion.1, f32[1,32,8,256]{3,2,1,0:T(8,128)S(1)} %get-tuple-element.42, ...), kind=kLoop, calls=%fused_computation.56 | loop fusion | flops 4980736 | bytes 13631488 | tf_op jit(solution)/shard_map/sub | solution.py:451
  96.1 0.0 all-to-all-done.spec
  96.1 0.0 copy-start.1
  96.1 1.0 copy-done.1
  97.1 23.1 %backward_exchange.1 = (f32[2,32,8,256]{3,2,1,0:T(8,128)}, f32[8,128]{1,0:T(8,128)}) custom-call(f32[32,32,256]{2,1,0:T(8,128)} %copy-done.1, f32[2,32,8,256]{3,2,1,0:T(8,128)} %fusion.30.v_rows, f32[8,128]{1,0:T(8,128)} %multiply_select_fusion.partial, bf16[256,1024]{1,0:T(8,128)(2,1)} %constant.168.clone.t_high, bf16[256,1024]{1,0:T(8,128)(2,1)} %constant.169.clone.t_low), custom_call_target="tpu_custom_call" | custom-call | tf_op jit(solution)/shard_map/backward_exchange/pallas_call | solution.py:423
  120.2 1.3 %slice_reduce_fusion = f32[2]{0:T(128)} fusion(f32[8,128]{1,0:T(8,128)} %get-tuple-element.19), kind=kLoop, calls=%fused_computation.301 | loop fusion | bytes 16 | tf_op jit(solution)/shard_map/slice | solution.py:475
  121.5 1.9 %copy.15 = f32[2,1,256,256]{3,2,1,0:T(8,128)} copy(f32[2,1,256,256]{3,2,1,0:T(8,128)} %bitcast.106) | data formatting | bytes 1048576
  (2 shorter events, 0.0 us)
Async XLA Ops:
  47.5 11.7 %collective-permute-start = (f32[2,32,4,256]{3,2,1,0:T(4,128)S(1)}, f32[2,32,4,256]{3,2,1,0:T(4,128)S(1)}, u32[]{:S(2)}, u32[]{:S(2)}) collective-permute-start(f32[2,32,4,256]{3,2,1,0:T(4,128)S(1)} %get-tuple-element.55), channel_id=1, source_target_pairs={{0,1},{1,2},{2,3},{3,4},{4,5},{5,6},{6,7},{7,8},{8,9},{9,10},{10,1... | collective-permute-start | bytes 786440 | tf_op jit(solution)/shard_map/ppermute | solution.py:27
  49.4 9.7 %collective-permute-start.1 = (f32[2,32,4,256]{3,2,1,0:T(4,128)S(1)}, f32[2,32,4,256]{3,2,1,0:T(4,128)S(1)}, u32[]{:S(2)}, u32[]{:S(2)}) collective-permute-start(f32[2,32,4,256]{3,2,1,0:T(4,128)S(1)} %get-tuple-element.56), channel_id=1, source_target_pairs={{1,0},{2,1},{3,2},{4,3},{5,4},{6,5},{7,6},{8,7},{9,8},{10,9},{11,1... | collective-permute-start | bytes 786440 | tf_op jit(solution)/shard_map/ppermute | solution.py:27
  51.8 7.3 %copy-start = (f32[2,32,8,256]{3,2,1,0:T(8,128)S(1)}, f32[2,32,8,256]{3,2,1,0:T(8,128)}, u32[]{:S(2)}) copy-start(f32[2,32,8,256]{3,2,1,0:T(8,128)} %get-tuple-element.15) | copy-start | bytes 1572868
  59.4 36.7 %all-to-all-start = ((f32[32,32,256]{2,1,0:T(8,128)}), f32[32,32,256]{2,1,0:T(8,128)S(1)}, u32[]{:S(2)}, u32[]{:S(2)}) async-start(f32[32,32,256]{2,1,0:T(8,128)} %get-tuple-element.14), calls=%async_computation | async-start | bytes 2097152 | tf_op jit(solution)/shard_map/all_to_all | solution.py:468
  78.6 9.5 %copy-start.2 = (f32[8,128]{1,0:T(8,128)S(1)}, f32[8,128]{1,0:T(8,128)}, u32[]{:S(2)}) copy-start(f32[8,128]{1,0:T(8,128)} %get-tuple-element.17) | copy-start | bytes 12292
  79.5 13.4 %collective-permute-start.2 = (f32[2,32,4,256]{3,2,1,0:T(4,128)}, f32[2,32,4,256]{3,2,1,0:T(4,128)}, u32[]{:S(2)}, u32[]{:S(2)}) collective-permute-start(f32[2,32,4,256]{3,2,1,0:T(4,128)} %get-tuple-element.51), channel_id=1, source_target_pairs={{1,0},{2,1},{3,2},{4,3},{5,4},{6,5},{7,6},{8,7},{9,8},{10,9},{11,1... | collective-permute-start | bytes 786440 | tf_op jit(solution)/shard_map/ppermute | solution.py:27
  81.8 11.1 %collective-permute-start.3 = (f32[2,32,4,256]{3,2,1,0:T(4,128)}, f32[2,32,4,256]{3,2,1,0:T(4,128)}, u32[]{:S(2)}, u32[]{:S(2)}) collective-permute-start(f32[2,32,4,256]{3,2,1,0:T(4,128)} %get-tuple-element.52), channel_id=1, source_target_pairs={{0,1},{1,2},{2,3},{3,4},{4,5},{5,6},{6,7},{7,8},{8,9},{9,10},{10,1... | collective-permute-start | bytes 786440 | tf_op jit(solution)/shard_map/ppermute | solution.py:27
  96.1 1.0 copy-start.1
where the time goes:
time: 124 us; the launch traced here: 123 us
  Pallas kernels  76 us (61%)
  other arithmetic  18.6 us (15%)
  starting transfers between devices  17.7 us (14%)
  local copies, waits for them, and re-layouts  5.44 us (4%)
  waiting for transfers between devices  4.15 us (3%)
  between operations  1.45 us (1%)
    pallas_call x1, Pallas kernels, forward_exchange(): pl.pallas_call(functools.partial(forward_kernel, devices), out_shape=(jax...  45.5 us
    pallas_call x1, Pallas kernels, backward_exchange(): pl.pallas_call(functools.partial(backward_kernel, devices), out_shape=(ja...  23.1 us
    ppermute x4, starting transfers between devices, shifted(): lax.ppermute(value, axis, [(source, source + steps) for source in range(l...  11.9 us
    pallas_call x1, Pallas kernels, filtered(): pl.pallas_call(filter_kernel, grid=(1,), out_shape=(jax.ShapeDtypeStruct(...  7.31 us
    all_to_all x1, starting transfers between devices, per_device(): back = lax.all_to_all(back, 'gz', split_axis=0, concat_axis=0, tiled=True)  5.84 us
    add_any x1, other arithmetic, energy_density(): up_cube = jnp.cbrt(2.0 * dens_up)  4.37 us
    ppermute x4, waiting for transfers between devices, shifted(): lax.ppermute(value, axis, [(source, source + steps) for source in range(l...  4.15 us
    reduce_sum x1, other arithmetic, xc_rows(): return (v_xc, jnp.sum(energy))  3.03 us
  transfers between devices with their start and end apart: 5, of which 1 were waited for; matrix products, arithmetic and copies ran while one was open for 15% of the time, Pallas kernels for 6%

commit v1 on v0

v1 whole, which is shorter than its diff:
```python
import functools
import math

import jax
import jax.numpy as jnp
import numpy as np
from jax import lax
from jax.experimental import pallas as pl
from jax.experimental.pallas import tpu as pltpu
from jax.sharding import PartitionSpec as P

HGRID = 0.35
STENCIL_WHOLE = (672.0, -168.0, 32.0, -3.0)
STENCIL_SCALE = 1.0 / (840.0 * HGRID)
REACH = len(STENCIL_WHOLE)
KAPPA = 0.804
MU_X = 0.2195149727645171
BETA_C = 0.06672455060314922
GAMMA_C = 0.031090690869654894
FZ_CURV = 1.709921
PARAMS_UNPOL = (0.031091, 0.2137, 7.5957, 3.5876, 1.6382, 0.49294)
PARAMS_POL = (0.015545, 0.20548, 14.1189, 6.1977, 3.3662, 0.62517)
PARAMS_STIFF = (0.016887, 0.11125, 10.357, 3.6231, 0.88026, 0.49671)

MESH = pl.DeviceIdType.MESH
LANES = 128
SUBLANES = 8
VMEM_SPEC = pl.BlockSpec(memory_space=pltpu.VMEM)
ANY_SPEC = pl.BlockSpec(memory_space=pl.ANY)
VMEM_BYTES = 60 * 1024 * 1024


def exchange_spin(dens, log_dens, sigma):
    factor = -0.75 * (3.0 / math.pi) ** (1.0 / 3.0) * 2.0 ** (1.0 / 3.0)
    scale = (3.0 * math.pi**2) ** (2.0 / 3.0) * 2.0 ** (8.0 / 3.0)
    inverse_cube = jnp.exp(log_dens * (-1.0 / 3.0))
    cube = dens * inverse_cube * inverse_cube
    product = dens * cube
    weight = product * product
    bent = (MU_X / (KAPPA * scale)) * sigma
    inverse = 1.0 / (weight + bent)
    share = weight * inverse
    rest = KAPPA * bent * inverse
    enhance = 1.0 + rest
    energy = factor * product * enhance
    by_dens = factor * cube * ((4.0 / 3.0) * enhance - (8.0 / 3.0) * rest * share)
    square = dens * dens * inverse
    by_sigma = (factor * MU_X / scale) * square * square
    return energy, by_dens, by_sigma, cube, inverse_cube


def pw_piece(root, square, params):
    amp, alpha, b1, b2, b3, b4 = params
    doubled = 2.0 * amp
    series = root * (doubled * b1 + root * (doubled * b2 + root * (doubled * b3 + root * (doubled * b4))))
    slope = doubled * b1 + root * (
        2.0 * doubled * b2 + root * (3.0 * doubled * b3 + root * (4.0 * doubled * b4))
    )
    above = series + 1.0
    inverse = 1.0 / (series * above)
    logarithm = jnp.log(above * above * inverse)
    front = -doubled - (doubled * alpha) * square
    value = front * logarithm
    by_root = (-2.0 * doubled * alpha) * root * logarithm - front * slope * inverse
    return value, by_root


def xc_point(up, down, sigma_uu, sigma_ud, sigma_dd):
    energy_u, vx_u, by_uu, cube_u, inverse_u = exchange_spin(up, jnp.log(up), sigma_uu)
    energy_d, vx_d, by_dd, cube_d, inverse_d = exchange_spin(down, jnp.log(down), sigma_dd)
    total = up + down
    sixth = jnp.exp(jnp.log(total) * (-1.0 / 6.0))
    inverse_cube = sixth * sixth
    wigner = (3.0 / (4.0 * math.pi)) ** (1.0 / 3.0)
    root = math.sqrt(wigner) * sixth
    square = wigner * inverse_cube
    inverse_square = inverse_cube * inverse_cube
    inverse_total = inverse_square * inverse_cube
    cube = total * inverse_square
    zeta = (up - down) * inverse_total
    plus = 1.0 + zeta
    minus = 1.0 - zeta
    third = 2.0 ** (1.0 / 3.0)
    plus_cube = third * cube_u * inverse_cube
    minus_cube = third * cube_d * inverse_cube
    spin = 1.0 / (2.0 ** (4.0 / 3.0) - 2.0)
    weight = (plus * plus_cube + minus * minus_cube - 2.0) * spin
    by_weight = (4.0 / 3.0 * spin) * (plus_cube - minus_cube)
    unpol, unpol_root = pw_piece(root, square, PARAMS_UNPOL)
    pol, pol_root = pw_piece(root, square, PARAMS_POL)
    stiff, stiff_root = pw_piece(root, square, PARAMS_STIFF)
    stiff = stiff * (-1.0 / FZ_CURV)
    stiff_root = stiff_root * (-1.0 / FZ_CURV)
    zeta_two = zeta * zeta
    zeta_four = zeta_two * zeta_two
    gap = pol - unpol - stiff
    mixed = stiff + gap * zeta_four
    mixed_root = stiff_root + (pol_root - unpol_root - stiff_root) * zeta_four
    local = unpol + weight * mixed
    local_root = unpol_root + weight * mixed_root
    local_zeta = by_weight * mixed + weight * gap * (4.0 * zeta_two * zeta)
    phi = 0.5 * (plus_cube * plus_cube + minus_cube * minus_cube)
    by_phi = (2.0 ** (-1.0 / 3.0) / 3.0) * cube * (inverse_u - inverse_d)
    inverse_phi = 1.0 / phi
    phi_square = inverse_phi * inverse_phi
    inverse_gamma = phi_square * inverse_phi * (1.0 / GAMMA_C)
    gamma_phi = GAMMA_C * phi * phi * phi
    ratio = BETA_C / GAMMA_C
    expo = -local * inverse_gamma
    weight_a = ratio / (jnp.exp(expo) - 1.0)
    scale = math.pi / (16.0 * (3.0 * math.pi**2) ** (1.0 / 3.0))
    to_t = scale * phi_square * (inverse_square * inverse_cube) * (inverse_square * inverse_square)
    sigma = sigma_uu + 2.0 * sigma_ud + sigma_dd
    tee = sigma * to_t
    why = weight_a * tee
    numer = 1.0 + why
    denom = 1.0 + why * numer
    scaled = ratio * tee
    upper = denom + scaled * numer
    inverse = 1.0 / (denom * upper)
    gradient = gamma_phi * jnp.log(upper * upper * inverse)
    shared = gamma_phi * inverse
    by_tee = ratio * shared * (numer + why)
    by_a = shared * scaled * tee * why * (numer + 1.0)
    chain = by_a * weight_a * (1.0 + weight_a * (1.0 / ratio))
    by_local = 1.0 - chain * inverse_gamma
    tee_part = tee * by_tee
    phi_part = (3.0 * gradient - 3.0 * expo * chain - 2.0 * tee_part) * inverse_phi
    corr = local + gradient
    by_total = corr - (1.0 / 6.0) * root * local_root * by_local - (7.0 / 3.0) * tee_part
    by_zeta = by_local * local_zeta + phi_part * by_phi
    by_sigma = total * by_tee * to_t
    energy = energy_u + energy_d + total * corr
    return (
        energy,
        vx_u + by_total + by_zeta * minus,
        vx_d + by_total - by_zeta * plus,
        by_uu + by_sigma,
        2.0 * by_sigma,
        by_dd + by_sigma,
    )


def np_split(table):
    table = np.asarray(table, np.float32)
    high = table.astype(jnp.bfloat16)
    low = (table - high.astype(np.float32)).astype(jnp.bfloat16)
    return high, low


def y_tables(width_y, devices, scale):
    period = 2 * width_y
    count = period // devices
    half = count // 2
    slots = max(half, SUBLANES)
    device = np.arange(devices)[:, None]
    ky = device * count + np.arange(half)[None, :] + (device >= devices // 2)
    space = np.arange(width_y)
    angle = (ky[:, :, None] * space % period) * (2.0 * np.pi / period)
    both = np.stack([np.cos(angle), -np.sin(angle)], axis=1)
    both[0, 1, 0] = (-1.0) ** space
    weight = np.full((devices, 2, half, 1), 2.0)
    weight[0, :, 0] = 1.0
    pad = [(0, 0), (0, 0), (0, slots - half), (0, 0)]
    forward = np.pad(both, pad).reshape(devices * 2 * slots, width_y)
    back = np.pad(both * weight, pad).reshape(devices * 2 * slots, width_y)
    return *np_split(forward), *np_split(back.T * scale)


def x_tables(width_x):
    index = np.outer(np.arange(width_x), np.arange(width_x)) % (2 * width_x)
    angle = index * (np.pi / width_x)
    cos, sin = np.cos(angle), np.sin(angle)
    sin[:, 0] = (-1.0) ** np.arange(width_x)
    fore = np.concatenate([cos, sin], axis=1)
    back = np.concatenate([cos, sin.T], axis=0)
    return *np_split(fore), *np_split(back)


def stencil_matrix(size):
    table = np.zeros((size, size + 2 * REACH), np.float32)
    for row in range(size):
        for step, weight in enumerate(STENCIL_WHOLE, 1):
            table[row, row + REACH + step] = weight
            table[row, row + REACH - step] = -weight
    return table


def slope_tables(width_x, rows):
    wide = stencil_matrix(width_x)[:, REACH : REACH + width_x].T
    table = stencil_matrix(rows)
    inner = table[:, REACH : REACH + rows]
    below, above = table[:, :REACH], table[:, REACH + rows :]
    pad = np.zeros((rows, -(rows + 2 * REACH) % 16), np.float32)
    tall = np.concatenate([inner, above, below, pad], axis=1)
    tall = np.concatenate([tall] * 3, axis=1)
    return wide.astype(jnp.bfloat16), tall.astype(jnp.bfloat16)


def turn_table(width_x):
    table = np.zeros((width_x, width_x), np.float32)
    lanes = np.arange(width_x)
    table[(width_x - lanes) % width_x, lanes] = 1.0
    return table.astype(jnp.bfloat16)


def dot(left, right):
    return jnp.dot(left, right, preferred_element_type=jnp.float32)


def split(value):
    high = value.astype(jnp.bfloat16)
    low = (value - high.astype(jnp.float32)).astype(jnp.bfloat16)
    return high, low


def split_three(value):
    high = value.astype(jnp.bfloat16)
    rest = value - high.astype(jnp.float32)
    middle = rest.astype(jnp.bfloat16)
    low = (rest - middle.astype(jnp.float32)).astype(jnp.bfloat16)
    return high, middle, low


def dot_exact(value, table):
    high, middle, low = split_three(value)
    return dot(high, table) + (dot(middle, table) + dot(low, table))


def add(left, right):
    if left is None or right is None:
        return left if right is None else right
    return left[0] + right[0], left[1] + right[1]


def sub(left, right):
    if right is None:
        return left
    return left[0] - right[0], left[1] - right[1]


def turn(value, numer, denom, sign):
    if value is None:
        return None
    numer = numer * sign % denom
    eighth = numer * 8
    re, im = value
    if eighth % (2 * denom) == 0:
        quarter = eighth // (2 * denom)
        return ((re, im), (-im, re), (-re, -im), (im, -re))[quarter]
    if eighth % denom == 0:
        root = math.sqrt(0.5)
        plus, minus = root * (re + im), root * (re - im)
        return {1: (minus, plus), 3: (-plus, minus), 5: (-minus, -plus), 7: (plus, -minus)}[eighth // denom]
    cos = math.cos(2.0 * math.pi * numer / denom)
    sin = math.sin(2.0 * math.pi * numer / denom)
    return cos * re - sin * im, sin * re + cos * im


def small_dft(values, sign, first_half=False):
    count = len(values)
    if count == 1:
        return values
    even = small_dft(values[0::2], sign)
    odd = small_dft(values[1::2], sign)
    odd = [turn(value, k, count, sign) for k, value in enumerate(odd)]
    out = [add(e, o) for e, o in zip(even, odd)]
    if not first_half:
        out += [sub(e, o) for e, o in zip(even, odd)]
    return out


class Copies:
    def __init__(self, sends, receives, index=None):
        self.sends, self.receives = sends, receives

    def make(self, source, target, send, receive, peer):
        return pltpu.make_async_remote_copy(
            src_ref=source,
            dst_ref=target,
            send_sem=self.sends.at[send],
            recv_sem=self.receives.at[receive],
            device_id=(peer,),
            device_id_type=MESH,
        )


def mega_kernel(
    devices,
    group,
    half,
    dens,
    ty_high,
    ty_low,
    khat_hbm,
    tb_high_hbm,
    tb_low_hbm,
    tx_high,
    tx_low,
    tr_high,
    tr_low,
    t_wide,
    t_tall,
    t_turn,
    out,
    e_out,
    khat,
    tb_high,
    tb_low,
    spec_out,
    spec_in,
    halo_out,
    halo_in,
    main,
    grad_x,
    grad_y,
    grad_z,
    flux_z,
    flux_out,
    flux_in,
    v_own,
    v_all,
    edge_out,
    edge_in,
    k_raw,
    k_self,
    k_cross,
    z_in,
    z_mid,
    h_spec,
    x_in,
    back_out,
    back_in,
    partial,
    sums,
    local_sems,
    spec_s,
    spec_r,
    back_s,
    back_r,
    part_s,
    part_r,
    main_s,
    main_r,
    halo_s,
    halo_r,
    fz_s,
    fz_r,
    fy_s,
    fy_r,
    v_s,
    v_r,
    edge_s,
    edge_r,
):
    me = lax.axis_index("gz")
    level, member = lax.div(me, group), lax.rem(me, group)
    levels = devices // group
    base = level * group
    width_y, width_x = dens.shape[1:]
    rows = width_y // group
    tiles = width_x // LANES
    depth = devices
    slots = spec_out.shape[1] // 2
    first_device, edge_device = 0, devices // 2
    cells = depth * width_y * width_x

    barrier = pltpu.get_barrier_semaphore()

    def greet(step, carry):
        pl.semaphore_signal(
            barrier, inc=1, device_id=(lax.rem(me + step, devices),), device_id_type=MESH
        )
        return carry

    lax.fori_loop(1, devices, greet, 0)

    locals_ = [
        pltpu.make_async_copy(source, target, local_sems.at[i])
        for i, (source, target) in enumerate(
            [(khat_hbm, khat), (tb_high_hbm, tb_high), (tb_low_hbm, tb_low)]
        )
    ]
    for copy in locals_:
        copy.start()

    def remote(source, target, send, receive, peer):
        return pltpu.make_async_remote_copy(
            src_ref=source,
            dst_ref=target,
            send_sem=send,
            recv_sem=receive,
            device_id=(peer,),
            device_id_type=MESH,
        )

    sub_row = lax.broadcasted_iota(jnp.int32, (1, SUBLANES, width_x), 1)
    for b in range(group):
        above = dens[:, (b + 1) * rows : (b + 1) * rows + SUBLANES] if b < group - 1 else 0.0
        below = dens[:, b * rows - SUBLANES : b * rows] if b else 0.0
        halo_out[b] = jnp.where(sub_row < REACH, above, below)

    total = dens[0] + dens[1]
    high, low = split(total)
    values = dot(ty_high[...], high) + (dot(ty_high[...], low) + dot(ty_low[...], high))
    spec_out[...] = values.reshape(spec_out.shape)

    pl.semaphore_wait(barrier, devices - 1)

    up = member >= group - REACH
    near = jnp.where(up, level + 1, level - 1)
    has_near = jnp.logical_and(near >= 0, near < levels)
    near_slot = jnp.where(up, member - (group - REACH), REACH + group + member)

    def block(b):
        return pl.ds(pl.multiple_of(b * rows, rows), rows)

    def main_copy(b, peer, slot, which):
        return remote(
            dens.at[:, block(b)], main.at[:, slot], main_s.at[which, b], main_r.at[slot], peer
        )

    def halo_copy(b, peer, source):
        return remote(
            halo_out.at[b], halo_in.at[source], halo_s.at[b], halo_r.at[source], peer
        )

    def in_group(act):
        def body(step, carry):
            b = lax.rem(member + step, group)
            act(b, base + b)
            return carry

        lax.fori_loop(1, group, body, 0)

    def start_main(b, peer):
        main_copy(b, peer, REACH + member, 0).start()
        halo_copy(b, peer, member).start()

    in_group(start_main)

    def near_each(act):
        @pl.when(has_near)
        def _():
            def body(step, carry):
                b = lax.rem(member + step, group)
                act(main_copy(b, near * group + b, near_slot, 1))
                return carry

            lax.fori_loop(0, group, body, 0)

    near_each(lambda copy: copy.start())

    def spec_copy(step, peer, slot):
        return remote(
            spec_out.at[peer], spec_in.at[slot], spec_s.at[step], spec_r.at[step], peer
        )

    def around(act):
        def body(step, carry):
            act(step, lax.rem(me + step, devices), lax.rem(me - step + devices, devices))
            return carry

        lax.fori_loop(1, devices, body, 0)

    around(lambda step, peer, origin: spec_copy(step, peer, me).start())
    main[:, REACH + member] = dens[:, block(member)]
    halo_in[member] = halo_out[member]
    spec_in[me] = spec_out[me]

    zero_planes = jnp.zeros((2, REACH, rows, width_x), jnp.float32)

    @pl.when(level == 0)
    def _():
        main[:, :REACH] = zero_planes
        flux_z[:, :REACH] = zero_planes

    @pl.when(level == levels - 1)
    def _():
        main[:, REACH + group :] = zero_planes
        flux_z[:, REACH + group :] = zero_planes

    locals_[0].wait()

    @pl.when(me == edge_device)
    def _():
        edge_out[...] = khat[:, 0, :]
        remote(edge_out, edge_in, edge_s, edge_r, first_device).start()

    lower = me < edge_device
    planes_k = khat.shape[0]
    if slots > half:
        k_raw[...] = jnp.ones(k_raw.shape, jnp.float32)

    def pick(kz, carry):
        row = jnp.where(lower, khat[kz, :half], khat[kz, 1 : half + 1])
        for t in range(tiles):
            k_self[kz, t, :half] = row[:, t * LANES : (t + 1) * LANES]
        k_raw[kz, :half] = row[:, width_x:]
        if slots > half:
            for t in range(tiles):
                k_self[kz, t, half:] = jnp.ones((slots - half, LANES), jnp.float32)
        return carry

    lax.fori_loop(0, planes_k, pick, 0)
    turned = dot_exact(k_raw[...].reshape(planes_k * slots, width_x), t_turn[...])
    turned = turned.reshape(planes_k, slots, width_x)
    for t in range(tiles):
        k_self[:, tiles + t] = turned[:, :, t * LANES : (t + 1) * LANES]

    def clear(kz, carry):
        k_cross[kz] = jnp.zeros(k_cross.shape[1:], jnp.float32)
        return carry

    lax.fori_loop(0, planes_k, clear, 0)

    @pl.when(me == first_device)
    def _():
        remote(edge_out, edge_in, edge_s, edge_r, edge_device).wait_recv()
        edge_out[:, :width_x] = edge_in[:, :width_x]
        edge_out[:, width_x:] = dot_exact(edge_in[:, width_x:], t_turn[...])
        top = lax.broadcasted_iota(jnp.int32, (slots, LANES), 0) == 0

        def mix(kz, carry):
            other = edge_out[pl.ds(kz, 1), :]
            for t in range(2 * tiles):
                mine = k_self[kz, t]
                theirs = other[:, t * LANES : (t + 1) * LANES]
                k_self[kz, t] = jnp.where(top, 0.5 * (mine + theirs), mine)
                k_cross[kz, t] = jnp.where(top, 0.5 * (mine - theirs), 0.0)
            return carry

        lax.fori_loop(0, planes_k, mix, 0)

    def finish_main(b, peer):
        main_copy(b, peer, REACH + b, 0).wait_recv()
        halo_copy(b, peer, b).wait_recv()

    in_group(finish_main)

    def near_wait(first):
        def body(step, carry):
            main_copy(member, me, first + step, 1).wait_recv()
            return carry

        lax.fori_loop(0, REACH, body, 0)

    @pl.when(level > 0)
    def _():
        near_wait(0)

    @pl.when(level < levels - 1)
    def _():
        near_wait(REACH + group)

    def slope_z(field, spin, plane):
        result = 0.0
        for step, weight in enumerate(STENCIL_WHOLE, 1):
            result = result + (weight * STENCIL_SCALE) * (
                field[spin, plane + REACH + step] - field[spin, plane + REACH - step]
            )
        return result

    pad_rows = t_tall.shape[1] // 3 - rows - SUBLANES

    def slope_y(inner, outer):
        parts = [inner, outer]
        if pad_rows:
            parts.append(jnp.zeros((pad_rows, width_x), jnp.float32))
        stacked = jnp.concatenate(split_three(jnp.concatenate(parts, axis=0)), axis=0)
        return dot(t_tall[...], stacked) * STENCIL_SCALE

    def slope_x(field):
        value = field.reshape(group * rows, width_x)
        return (dot_exact(value, t_wide[...]) * STENCIL_SCALE).reshape(group, rows, width_x)

    for spin in range(2):
        grad_x[spin] = slope_x(main[spin, REACH : REACH + group])

    def gradients(plane, carry):
        for spin in range(2):
            grad_z[spin, plane] = slope_z(main, spin, plane)
            grad_y[spin, plane] = slope_y(main[spin, REACH + plane], halo_in[plane, spin])
        return carry

    lax.fori_loop(0, group, gradients, 0)

    chunk = SUBLANES

    def point(index, acc):
        plane = lax.div(index, rows // chunk)
        at = pl.ds(pl.multiple_of(lax.rem(index, rows // chunk) * chunk, chunk), chunk)
        uz, uy, ux = grad_z[0, plane, at], grad_y[0, plane, at], grad_x[0, plane, at]
        dz, dy, dx = grad_z[1, plane, at], grad_y[1, plane, at], grad_x[1, plane, at]
        energy, d_up, d_down, d_uu, d_ud, d_dd = xc_point(
            main[0, REACH + plane, at],
            main[1, REACH + plane, at],
            uz * uz + uy * uy + ux * ux,
            uz * dz + uy * dy + ux * dx,
            dz * dz + dy * dy + dx * dx,
        )
        v_own[0, plane, at] = d_up
        v_own[1, plane, at] = d_down
        d_uu = 2.0 * d_uu
        d_dd = 2.0 * d_dd
        flux_z[0, REACH + plane, at] = d_uu * uz + d_ud * dz
        flux_z[1, REACH + plane, at] = d_dd * dz + d_ud * uz
        grad_y[0, plane, at] = d_uu * uy + d_ud * dy
        grad_y[1, plane, at] = d_dd * dy + d_ud * uy
        grad_x[0, plane, at] = d_uu * ux + d_ud * dx
        grad_x[1, plane, at] = d_dd * dx + d_ud * ux
        return acc + energy

    energy_acc = lax.fori_loop(
        0, group * rows // chunk, point, jnp.zeros((chunk, width_x), jnp.float32)
    )
    energy_xc = jnp.sum(energy_acc) * (1.0 / cells)

    def flux_z_copy(side, peer):
        source = (slice(group, group + REACH), slice(REACH, 2 * REACH))[side]
        target = (slice(0, REACH), slice(REACH + group, 2 * REACH + group))[side]
        return remote(
            flux_z.at[:, source], flux_z.at[:, target], fz_s.at[side], fz_r.at[side], peer
        )

    def flux_y_copy(side, peer):
        return remote(flux_out, flux_in.at[side], fy_s.at[side], fy_r.at[side], peer)

    exists_up, exists_down = level < levels - 1, level > 0
    right, left = member < group - 1, member > 0

    @pl.when(exists_up)
    def _():
        flux_z_copy(0, me + group).start()

    @pl.when(exists_down)
    def _():
        flux_z_copy(1, me - group).start()

    for spin in range(2):
        flux_out[:, spin] = jnp.where(
            sub_row < REACH, grad_y[spin, :, :SUBLANES], grad_y[spin, :, rows - SUBLANES :]
        )

    @pl.when(right)
    def _():
        flux_y_copy(0, me + 1).start()

    @pl.when(left)
    def _():
        flux_y_copy(1, me - 1).start()

    around(lambda step, peer, origin: spec_copy(step, peer, origin).wait_recv())
    lane = lax.broadcasted_iota(jnp.int32, (1, 1, width_x), 2)
    first = lane == 0
    high, low = split(spec_in[...].reshape(depth * 2 * slots, width_x))
    wide = dot(high, tx_high[...]) + (dot(low, tx_high[...]) + dot(high, tx_low[...]))
    wide = wide.reshape(depth, 2, slots, 2 * width_x)
    cos_re, cos_im = wide[:, 0, :, :width_x], wide[:, 1, :, :width_x]
    sin_re, sin_im = wide[:, 0, :, width_x:], wide[:, 1, :, width_x:]
    fields = (
        (jnp.where(first, cos_re, cos_re + sin_im), jnp.where(first, cos_im, cos_im - sin_re)),
        (jnp.where(first, sin_re, cos_re - sin_im), jnp.where(first, sin_im, cos_im + sin_re)),
    )
    for sign in range(2):
        for part in range(2):
            for t in range(tiles):
                z_in[:, part, sign * tiles + t] = fields[sign][part][
                    :, :, t * LANES : (t + 1) * LANES
                ]

    n1, n2 = z_mid.shape[:2]
    full = n1 * n2

    def load(ref, *at):
        return ref[at[0], 0, at[1]], ref[at[0], 1, at[1]]

    def fore(col, carry):
        for j in range(n2):
            given = [load(z_in, n2 * i + j, col) for i in range(n1 // 2)]
            for k, value in enumerate(small_dft(given + [None] * (n1 // 2), -1)):
                re, im = turn(value, k * j, full, -1)
                z_mid[k, j, 0] = re
                z_mid[k, j, 1] = im
        for k in range(n1):
            given = [(z_mid[k, j, 0], z_mid[k, j, 1]) for j in range(n2)]
            for m, (re, im) in enumerate(small_dft(given, -1)):
                h_spec[k + n1 * m, 0, col] = re
                h_spec[k + n1 * m, 1, col] = im
        return carry

    lax.fori_loop(0, 2 * tiles, fore, 0)
    lane = lax.broadcasted_iota(jnp.int32, (slots, LANES), 1)

    def back(col, carry):
        other = lax.rem(col + tiles, 2 * tiles)
        alone = jnp.logical_and(lane == 0, lax.rem(col, tiles) == 0)
        for k in range(n1):
            given = []
            for m in range(n2):
                kz = k + n1 * m
                flip = (full - kz) % full
                re, im = load(h_spec, kz, col)
                own_re, own_im = load(h_spec, flip, col)
                far_re, far_im = load(h_spec, flip, other)
                far_re = jnp.where(alone, own_re, far_re)
                far_im = jnp.where(alone, own_im, far_im)
                direct, cross = k_self[kz, col], k_cross[kz, col]
                given.append((direct * re + cross * far_re, direct * im - cross * far_im))
            for j, value in enumerate(small_dft(given, 1)):
                re, im = turn(value, k * j, full, 1)
                z_mid[k, j, 0] = re
                z_mid[k, j, 1] = im
        for j in range(n2):
            given = [(z_mid[k, j, 0], z_mid[k, j, 1]) for k in range(n1)]
            for i, (re, im) in enumerate(small_dft(given, 1, first_half=True)):
                z_in[n2 * i + j, 0, col] = re
                z_in[n2 * i + j, 1, col] = im
        return carry

    lax.fori_loop(0, 2 * tiles, back, 0)
    for t in range(tiles):
        keep = lax.broadcasted_iota(jnp.int32, (1, 1, LANES), 2) + t * LANES == 0
        plus_re, plus_im = z_in[:, 0, t], z_in[:, 1, t]
        minus_re, minus_im = z_in[:, 0, tiles + t], z_in[:, 1, tiles + t]
        here = slice(t * LANES, (t + 1) * LANES)
        there = slice(width_x + t * LANES, width_x + (t + 1) * LANES)
        x_in[:, 0, :, here] = jnp.where(keep, plus_re, plus_re + minus_re)
        x_in[:, 1, :, here] = jnp.where(keep, plus_im, plus_im + minus_im)
        x_in[:, 0, :, there] = jnp.where(keep, minus_re, minus_im - plus_im)
        x_in[:, 1, :, there] = jnp.where(keep, minus_im, plus_re - minus_re)
    high, low = split(x_in[...].reshape(depth * 2 * slots, 2 * width_x))
    values = dot(high, tr_high[...]) + (dot(low, tr_high[...]) + dot(high, tr_low[...]))
    back_out[...] = values.reshape(back_out.shape)

    def back_copy(step, peer, slot):
        return remote(
            back_out.at[peer], back_in.at[slot], back_s.at[step], back_r.at[step], peer
        )

    around(lambda step, peer, origin: back_copy(step, peer, me).start())
    back_in[me] = back_out[me]

    acc = jnp.sum(spec_in[...] * back_out[...], axis=0)
    row = lax.broadcasted_iota(jnp.int32, acc.shape, 0)
    single = jnp.logical_and(me == first_device, lax.rem(row, slots) == 0)
    energy_h = jnp.sum(jnp.where(single, acc, 2.0 * acc)) * (0.5 / (8.0 * cells) / cells)
    row = lax.broadcasted_iota(jnp.int32, partial.shape, 0)
    partial[...] = jnp.where(row == 0, energy_xc, energy_h)

    def part_copy(step, peer, slot):
        return remote(partial, sums.at[slot], part_s.at[step], part_r.at[step], peer)

    around(lambda step, peer, origin: part_copy(step, peer, me).start())
    sums[me] = partial[...]

    @pl.when(exists_down)
    def _():
        flux_z_copy(0, me).wait_recv()

    @pl.when(exists_up)
    def _():
        flux_z_copy(1, me).wait_recv()

    @pl.when(left)
    def _():
        flux_y_copy(0, me).wait_recv()

    @pl.when(right)
    def _():
        flux_y_copy(1, me).wait_recv()

    @pl.when(jnp.logical_not(left))
    def _():
        flux_in[0] = jnp.zeros(flux_in.shape[1:], jnp.float32)

    @pl.when(jnp.logical_not(right))
    def _():
        flux_in[1] = jnp.zeros(flux_in.shape[1:], jnp.float32)

    for spin in range(2):
        v_own[spin] = v_own[spin] - slope_x(grad_x[spin])

    def divergence(plane, carry):
        for spin in range(2):
            outer = jnp.where(sub_row[0] < REACH, flux_in[1, plane, spin], flux_in[0, plane, spin])
            v_own[spin, plane] = v_own[spin, plane] - (
                slope_z(flux_z, spin, plane) + slope_y(grad_y[spin, plane], outer)
            )
        return carry

    lax.fori_loop(0, group, divergence, 0)

    def v_copy(b, peer, source):
        return remote(
            v_own.at[:, b], v_all.at[:, block(source)], v_s.at[b], v_r.at[source], peer
        )

    in_group(lambda b, peer: v_copy(b, peer, member).start())
    v_all[:, block(member)] = v_own[:, member]

    locals_[1].wait()
    locals_[2].wait()
    around(lambda step, peer, origin: back_copy(step, peer, origin).wait_recv())
    high, low = split(back_in[...].reshape(depth * 2 * slots, width_x))
    hartree = dot(tb_high[...], high) + (dot(tb_high[...], low) + dot(tb_low[...], high))
    in_group(lambda b, peer: v_copy(b, peer, b).wait_recv())
    out[0] = hartree + v_all[0]
    out[1] = hartree + v_all[1]
    around(lambda step, peer, origin: part_copy(step, peer, origin).wait_recv())
    e_out[...] = jnp.sum(sums[...], axis=0)

    def sent(b, peer):
        main_copy(b, peer, REACH + member, 0).wait_send()
        halo_copy(b, peer, member).wait_send()
        v_copy(b, peer, member).wait_send()

    in_group(sent)
    near_each(lambda copy: copy.wait_send())

    def sent_around(step, peer, origin):
        spec_copy(step, peer, me).wait_send()
        back_copy(step, peer, me).wait_send()
        part_copy(step, peer, me).wait_send()

    around(sent_around)

    @pl.when(exists_up)
    def _():
        flux_z_copy(0, me + group).wait_send()

    @pl.when(exists_down)
    def _():
        flux_z_copy(1, me - group).wait_send()

    @pl.when(right)
    def _():
        flux_y_copy(0, me + 1).wait_send()

    @pl.when(left)
    def _():
        flux_y_copy(1, me - 1).wait_send()

    @pl.when(me == edge_device)
    def _():
        remote(edge_out, edge_in, edge_s, edge_r, first_device).wait_send()


def per_device(density, kernel_hat):
    planes, width_y, width_x = density.shape[1:]
    devices = lax.axis_size("gz")
    assert planes == 1
    group = 2 * REACH
    rows = width_y // group
    cells = devices * width_y * width_x
    count = kernel_hat.shape[1]
    half = count // 2
    slots = max(half, SUBLANES)
    tiles = width_x // LANES
    full = 2 * devices
    n1 = 1 << (full.bit_length() // 2)
    ty_high, ty_low, tb_high, tb_low = y_tables(width_y, devices, 1.0 / (8 * cells))
    x_parts = x_tables(width_x)
    t_wide, t_tall = slope_tables(width_x, rows)
    spec_shape = (devices, 2 * slots, width_x)
    tile_shape = (2, group, rows, width_x)
    tall_shape = (2, group + 2 * REACH, rows, width_x)
    f32 = functools.partial(pltpu.VMEM, dtype=jnp.float32)
    dma = pltpu.SemaphoreType.DMA
    scratch = [
        f32(kernel_hat.shape),
        pltpu.VMEM(tb_high.shape, jnp.bfloat16),
        pltpu.VMEM(tb_low.shape, jnp.bfloat16),
        f32(spec_shape),
        f32(spec_shape),
        f32((group, 2, SUBLANES, width_x)),
        f32((group, 2, SUBLANES, width_x)),
        f32(tall_shape),
        f32(tile_shape),
        f32(tile_shape),
        f32(tile_shape),
        f32(tall_shape),
        f32((group, 2, SUBLANES, width_x)),
        f32((2, group, 2, SUBLANES, width_x)),
        f32(tile_shape),
        f32((2, width_y, width_x)),
        f32((full, 2 * width_x)),
        f32((full, 2 * width_x)),
        f32((full, slots, width_x)),
        f32((full, 2 * tiles, slots, LANES)),
        f32((full, 2 * tiles, slots, LANES)),
        f32((devices, 2, 2 * tiles, slots, LANES)),
        f32((n1, full // n1, 2, slots, LANES)),
        f32((full, 2, 2 * tiles, slots, LANES)),
        f32((devices, 2, slots, 2 * width_x)),
        f32(spec_shape),
        f32(spec_shape),
        f32((SUBLANES, LANES)),
        f32((devices, SUBLANES, LANES)),
        dma((3,)),
        dma((devices,)),
        dma((devices,)),
        dma((devices,)),
        dma((devices,)),
        dma((devices,)),
        dma((devices,)),
        dma((2, group)),
        dma((group + 2 * REACH,)),
        dma((group,)),
        dma((group,)),
        dma((2,)),
        dma((2,)),
        dma((2,)),
        dma((2,)),
        dma((group,)),
        dma((group,)),
        dma,
        dma,
    ]
    potential, energies = pl.pallas_call(
        functools.partial(mega_kernel, devices, group, half),
        out_shape=(
            jax.ShapeDtypeStruct((2, width_y, width_x), jnp.float32),
            jax.ShapeDtypeStruct((SUBLANES, LANES), jnp.float32),
        ),
        in_specs=[VMEM_SPEC] * 3 + [ANY_SPEC] * 3 + [VMEM_SPEC] * 7,
        out_specs=(VMEM_SPEC, VMEM_SPEC),
        scratch_shapes=scratch,
        compiler_params=pltpu.CompilerParams(
            collective_id=0, has_side_effects=True, vmem_limit_bytes=VMEM_BYTES
        ),
        name="potential",
    )(
        density.reshape(2, width_y, width_x),
        ty_high,
        ty_low,
        kernel_hat,
        tb_high,
        tb_low,
        *x_parts,
        t_wide,
        t_tall,
        turn_table(width_x),
    )
    return potential.reshape(density.shape), energies[:2, 0]


def solution(mesh):
    placed = (P(None, "gz", None, None), P(None, "gz", None))
    return jax.shard_map(
        per_device,
        mesh=mesh,
        in_specs=placed,
        out_specs=(P(None, "gz", None, None), P()),
        check_vma=False,
    )
```

time: 124 us -> 63.1 us (0.51)
  the two profiles are of different devices: /device:TPU:15 before, /device:TPU:0 now
where the time goes in v1:
time: 63.1 us; the launch traced here: 62.9 us
  Pallas kernels  59 us (94%)
  local copies, waits for them, and re-layouts  3.18 us (5%)
  between operations  0.64 us (1%)
    pallas_call x1, Pallas kernels, per_device(): pl.pallas_call(functools.partial(mega_kernel, devices, group, half), out_...  59 us
    unnamed x1, local copies, waits for them, and re-layouts  1.87 us
    slice x1, local copies, waits for them, and re-layouts, per_device(): return (potential.reshape(density.shape), energies[:2, 0])  1.31 us

profile of v1, /device:TPU:0, one launch (start us, length us, event | category | flops | bytes accessed | tf_op | source)
XLA Modules:
  0.0 62.9 jit_solution(13267560478654398622)
XLA Ops:
  0.6 59.0 %potential.1 = (f32[2,256,256]{2,1,0:T(8,128)}, f32[8,128]{1,0:T(8,128)}) custom-call(f32[2,256,256]{2,1,0:T(8,128)} %bitcast.4, bf16[512,256]{1,0:T(8,128)(2,1)} %constant.22.clone.ty_high, bf16[512,256]{1,0:T(8,128)(2,1)} %constant.23.clone.ty_low, f32[64,16,512]{2,1,0:T(8,128)} %khat_hbm.1, bf16[256,512]{1,0:T(8,128)(2,1)} %constant.24.clone.tb_high_hbm, ...), custom_call_target="tpu_custom_call" | custom-call | tf_op jit(solution)/shard_map/potential/pallas_call | solution.py:920
  59.7 1.3 %slice_reduce_fusion = f32[2]{0:T(128)} fusion(f32[8,128]{1,0:T(8,128)} %get-tuple-element.5), kind=kLoop, calls=%fused_computation | loop fusion | bytes 16 | tf_op jit(solution)/shard_map/slice | solution.py:945
  61.0 1.9 %copy.18 = f32[2,1,256,256]{3,2,1,0:T(8,128)} copy(f32[2,1,256,256]{3,2,1,0:T(8,128)} %bitcast.5) | data formatting | bytes 1048576

commit v2 on v1

--- a/solution.py
+++ b/solution.py
@@ -25,9 +25,12 @@
 MESH = pl.DeviceIdType.MESH
 LANES = 128
 SUBLANES = 8
+PACK = 256
 VMEM_SPEC = pl.BlockSpec(memory_space=pltpu.VMEM)
-ANY_SPEC = pl.BlockSpec(memory_space=pl.ANY)
-VMEM_BYTES = 60 * 1024 * 1024
+HBM_SPEC = pl.BlockSpec(memory_space=pltpu.HBM)
+VMEM_BYTES = 52 * 1024 * 1024
+VMEM_MOST = 63 * 1024 * 1024
+EARLY = 8
 
 
 def exchange_spin(dens, log_dens, sigma):
@@ -194,6 +197,7 @@
     pad = np.zeros((rows, -(rows + 2 * REACH) % 16), np.float32)
     tall = np.concatenate([inner, above, below, pad], axis=1)
     tall = np.concatenate([tall] * 3, axis=1)
+    tall = np.pad(tall, [(0, 0), (0, -tall.shape[1] % PACK)])
     return wide.astype(jnp.bfloat16), tall.astype(jnp.bfloat16)
 
 
@@ -202,6 +206,18 @@
     lanes = np.arange(width_x)
     table[(width_x - lanes) % width_x, lanes] = 1.0
     return table.astype(jnp.bfloat16)
+
+
+def pack(tables):
+    blocks, places, row = [], [], 0
+    for table in tables:
+        starts = []
+        for column in range(0, table.shape[1], PACK):
+            starts.append(row)
+            blocks.append(table[:, column : column + PACK])
+            row += table.shape[0]
+        places.append((table.shape[0], tuple(starts)))
+    return np.concatenate(blocks, axis=0), tuple(places)
 
 
 def dot(left, right):
@@ -270,89 +286,60 @@
     return out
 
 
-class Copies:
-    def __init__(self, sends, receives, index=None):
-        self.sends, self.receives = sends, receives
-
-    def make(self, source, target, send, receive, peer):
-        return pltpu.make_async_remote_copy(
-            src_ref=source,
-            dst_ref=target,
-            send_sem=self.sends.at[send],
-            recv_sem=self.receives.at[receive],
-            device_id=(peer,),
-            device_id_type=MESH,
-        )
-
-
 def mega_kernel(
     devices,
     group,
     half,
-    dens,
-    ty_high,
-    ty_low,
-    khat_hbm,
-    tb_high_hbm,
-    tb_low_hbm,
-    tx_high,
-    tx_low,
-    tr_high,
-    tr_low,
-    t_wide,
-    t_tall,
-    t_turn,
-    out,
-    e_out,
-    khat,
-    tb_high,
-    tb_low,
-    spec_out,
-    spec_in,
-    halo_out,
-    halo_in,
-    main,
-    grad_x,
-    grad_y,
-    grad_z,
-    flux_z,
-    flux_out,
-    flux_in,
-    v_own,
-    v_all,
-    edge_out,
-    edge_in,
-    k_raw,
-    k_self,
-    k_cross,
-    z_in,
-    z_mid,
-    h_spec,
-    x_in,
-    back_out,
-    back_in,
-    partial,
-    sums,
-    local_sems,
-    spec_s,
-    spec_r,
-    back_s,
-    back_r,
-    part_s,
-    part_r,
-    main_s,
-    main_r,
-    halo_s,
-    halo_r,
-    fz_s,
-    fz_r,
-    fy_s,
-    fy_r,
-    v_s,
-    v_r,
-    edge_s,
-    edge_r,
+    places,
+    *refs,
 ):
+    dens_hbm, khat_hbm, table_hbm, hartree, v_all, sums, dens, khat, table = refs[:9]
+    (
+        spec_out,
+        spec_in,
+        halo_out,
+        halo_in,
+        main,
+        grad_x,
+        grad_y,
+        grad_z,
+        flux_z,
+        flux_out,
+        flux_in,
+        v_own,
+        edge_out,
+        edge_in,
+        k_raw,
+        k_self,
+        k_cross,
+        z_in,
+        z_mid,
+        h_spec,
+        x_in,
+        back_out,
+        back_in,
+        partial,
+        local_sems,
+        spec_s,
+        spec_r,
+        back_s,
+        back_r,
+        part_s,
+        part_r,
+        main_s,
+        main_r,
+        relay_s,
+        halo_s,
+        halo_r,
+        fz_s,
+        fz_r,
+        fy_s,
+        fy_r,
+        v_s,
+        v_r,
+        edge_s,
+        edge_r,
+    ) = refs[9:]
     me = lax.axis_index("gz")
     level, member = lax.div(me, group), lax.rem(me, group)
     levels = devices // group
@@ -375,14 +362,36 @@
 
     lax.fori_loop(1, devices, greet, 0)
 
-    locals_ = [
+    cuts = (0, places[2][1][0], places[5][1][0], table.shape[0])
+    pairs = [(dens_hbm, dens)]
+    pairs += [
+        (table_hbm.at[low:high], table.at[low:high]) for low, high in zip(cuts, cuts[1:])
+    ]
+    pairs.insert(2, (khat_hbm, khat))
+    loads = [
         pltpu.make_async_copy(source, target, local_sems.at[i])
-        for i, (source, target) in enumerate(
-            [(khat_hbm, khat), (tb_high_hbm, tb_high), (tb_low_hbm, tb_low)]
-        )
+        for i, (source, target) in enumerate(pairs)
     ]
-    for copy in locals_:
+    for copy in loads:
         copy.start()
+
+    def blocks(index):
+        count, starts = places[index]
+        return [table[start : start + count] for start in starts]
+
+    def from_left(index, high, low):
+        result = 0.0
+        for k, (t_high, t_low) in enumerate(zip(blocks(index), blocks(index + 1))):
+            part = slice(k * PACK, k * PACK + t_high.shape[1])
+            upper, lower = high[part], low[part]
+            result = result + (dot(t_high, upper) + (dot(t_high, lower) + dot(t_low, upper)))
+        return result
+
+    def from_right(index, high, low):
+        return [
+            dot(high, t_high) + (dot(low, t_high) + dot(high, t_low))
+            for t_high, t_low in zip(blocks(index), blocks(index + 1))
+        ]
 
     def remote(source, target, send, receive, peer):
         return pltpu.make_async_remote_copy(
@@ -394,35 +403,37 @@
             device_id_type=MESH,
         )
 
+    loads[0].wait()
     sub_row = lax.broadcasted_iota(jnp.int32, (1, SUBLANES, width_x), 1)
     for b in range(group):
         above = dens[:, (b + 1) * rows : (b + 1) * rows + SUBLANES] if b < group - 1 else 0.0
         below = dens[:, b * rows - SUBLANES : b * rows] if b else 0.0
         halo_out[b] = jnp.where(sub_row < REACH, above, below)
 
-    total = dens[0] + dens[1]
-    high, low = split(total)
-    values = dot(ty_high[...], high) + (dot(ty_high[...], low) + dot(ty_low[...], high))
-    spec_out[...] = values.reshape(spec_out.shape)
-
     pl.semaphore_wait(barrier, devices - 1)
 
-    up = member >= group - REACH
-    near = jnp.where(up, level + 1, level - 1)
+    upper = member >= REACH
+    own_half = jnp.where(upper, REACH, 0)
+    far_half = REACH - own_half
+    near = jnp.where(upper, level + 1, level - 1)
+    relay = jnp.where(upper, level - 1, level + 1)
     has_near = jnp.logical_and(near >= 0, near < levels)
-    near_slot = jnp.where(up, member - (group - REACH), REACH + group + member)
+    has_relay = jnp.logical_and(relay >= 0, relay < levels)
+
+    def beyond(plane):
+        return jnp.where(plane >= REACH, plane - (group - REACH), REACH + group + plane)
 
     def block(b):
         return pl.ds(pl.multiple_of(b * rows, rows), rows)
 
     def main_copy(b, peer, slot, which):
         return remote(
-            dens.at[:, block(b)], main.at[:, slot], main_s.at[which, b], main_r.at[slot], peer
+            dens.at[:, block(b)], main.at[:, slot], main_s.at[which], main_r.at[slot], peer
         )
 
     def halo_copy(b, peer, source):
         return remote(
-            halo_out.at[b], halo_in.at[source], halo_s.at[b], halo_r.at[source], peer
+            halo_out.at[b], halo_in.at[source], halo_s, halo_r, peer
         )
 
     def in_group(act):
@@ -437,33 +448,69 @@
         main_copy(b, peer, REACH + member, 0).start()
         halo_copy(b, peer, member).start()
 
-    in_group(start_main)
-
     def near_each(act):
         @pl.when(has_near)
         def _():
             def body(step, carry):
-                b = lax.rem(member + step, group)
-                act(main_copy(b, near * group + b, near_slot, 1))
+                b = own_half + lax.rem(member + step, REACH)
+                act(main_copy(b, near * group + b, beyond(member), 1))
                 return carry
 
-            lax.fori_loop(0, group, body, 0)
+            lax.fori_loop(0, REACH, body, 0)
+
+    def relay_copy(step):
+        plane = far_half + lax.rem(member + REACH - step, REACH)
+        return plane, remote(
+            main.at[:, REACH + plane],
+            main.at[:, beyond(plane)],
+            relay_s,
+            main_r.at[beyond(plane)],
+            relay * group + member,
+        )
 
     near_each(lambda copy: copy.start())
+
+    def start_far(step, carry):
+        b = far_half + lax.rem(member + step, REACH)
+        start_main(b, base + b)
+        return carry
+
+    def start_own(step, carry):
+        b = own_half + lax.rem(member + step, REACH)
+        start_main(b, base + b)
+        return carry
+
+    lax.fori_loop(0, REACH, start_far, 0)
+    lax.fori_loop(1, REACH, start_own, 0)
+
+    loads[1].wait()
+    high, low = split(dens[0] + dens[1])
+    spec_out[...] = from_left(0, high, low).reshape(spec_out.shape)
+    loads[2].wait()
+
+    @pl.when(me == edge_device)
+    def _():
+        edge_out[...] = khat[:, 0, :]
+        remote(edge_out, edge_in, edge_s, edge_r, first_device).start()
 
     def spec_copy(step, peer, slot):
         return remote(
-            spec_out.at[peer], spec_in.at[slot], spec_s.at[step], spec_r.at[step], peer
+            spec_out.at[peer], spec_in.at[slot], spec_s, spec_r, peer
         )
 
-    def around(act):
-        def body(step, carry):
+    def around(act, first=1, last=devices):
+        def body(index, carry):
+            away = lax.div(index, 2)
+            step = devices // 2 + jnp.where(lax.rem(index, 2) == 0, away, -away)
             act(step, lax.rem(me + step, devices), lax.rem(me - step + devices, devices))
             return carry
 
-        lax.fori_loop(1, devices, body, 0)
-
-    around(lambda step, peer, origin: spec_copy(step, peer, me).start())
+        lax.fori_loop(first, last, body, 0)
+
+    def start_spec(step, peer, origin):
+        spec_copy(step, peer, me).start()
+
+    around(start_spec, last=1 + EARLY)
     main[:, REACH + member] = dens[:, block(member)]
     halo_in[member] = halo_out[member]
     spec_in[me] = spec_out[me]
@@ -480,13 +527,8 @@
         main[:, REACH + group :] = zero_planes
         flux_z[:, REACH + group :] = zero_planes
 
-    locals_[0].wait()
-
-    @pl.when(me == edge_device)
-    def _():
-        edge_out[...] = khat[:, 0, :]
-        remote(edge_out, edge_in, edge_s, edge_r, first_device).start()
-
+    loads[3].wait()
+    (t_turn,), (t_wide,), (t_tall,) = blocks(2), blocks(3), blocks(4)
     lower = me < edge_device
     planes_k = khat.shape[0]
     if slots > half:
@@ -503,7 +545,7 @@
         return carry
 
     lax.fori_loop(0, planes_k, pick, 0)
-    turned = dot_exact(k_raw[...].reshape(planes_k * slots, width_x), t_turn[...])
+    turned = dot_exact(k_raw[...].reshape(planes_k * slots, width_x), t_turn)
     turned = turned.reshape(planes_k, slots, width_x)
     for t in range(tiles):
         k_self[:, tiles + t] = turned[:, :, t * LANES : (t + 1) * LANES]
@@ -514,44 +556,30 @@
 
     lax.fori_loop(0, planes_k, clear, 0)
 
-    @pl.when(me == first_device)
-    def _():
-        remote(edge_out, edge_in, edge_s, edge_r, edge_device).wait_recv()
-        edge_out[:, :width_x] = edge_in[:, :width_x]
-        edge_out[:, width_x:] = dot_exact(edge_in[:, width_x:], t_turn[...])
-        top = lax.broadcasted_iota(jnp.int32, (slots, LANES), 0) == 0
-
-        def mix(kz, carry):
-            other = edge_out[pl.ds(kz, 1), :]
-            for t in range(2 * tiles):
-                mine = k_self[kz, t]
-                theirs = other[:, t * LANES : (t + 1) * LANES]
-                k_self[kz, t] = jnp.where(top, 0.5 * (mine + theirs), mine)
-                k_cross[kz, t] = jnp.where(top, 0.5 * (mine - theirs), 0.0)
-            return carry
-
-        lax.fori_loop(0, planes_k, mix, 0)
-
     def finish_main(b, peer):
         main_copy(b, peer, REACH + b, 0).wait_recv()
-        halo_copy(b, peer, b).wait_recv()
-
-    in_group(finish_main)
-
-    def near_wait(first):
-        def body(step, carry):
-            main_copy(member, me, first + step, 1).wait_recv()
-            return carry
-
-        lax.fori_loop(0, REACH, body, 0)
-
-    @pl.when(level > 0)
-    def _():
-        near_wait(0)
-
-    @pl.when(level < levels - 1)
-    def _():
-        near_wait(REACH + group)
+
+    def finish_far(step, carry):
+        plane, copy = relay_copy(step)
+        finish_main(plane, base + plane)
+
+        @pl.when(has_relay)
+        def _():
+            copy.start()
+
+        return carry
+
+    lax.fori_loop(0, REACH, finish_far, 0)
+    around(start_spec, first=1 + EARLY)
+
+    def finish_own(step, carry):
+        b = own_half + lax.rem(member + step, REACH)
+        finish_main(b, base + b)
+        return carry
+
+    lax.fori_loop(1, REACH, finish_own, 0)
+    mates = pl.ds(0, group - 1)
+    remote(halo_out.at[mates], halo_in.at[mates], halo_s, halo_r, me).wait_recv()
 
     def slope_z(field, spin, plane):
         result = 0.0
@@ -561,29 +589,51 @@
             )
         return result
 
-    pad_rows = t_tall.shape[1] // 3 - rows - SUBLANES
+    pad_rows = -(rows + SUBLANES) % 16
+    tall = 3 * (rows + SUBLANES + pad_rows)
 
     def slope_y(inner, outer):
         parts = [inner, outer]
         if pad_rows:
             parts.append(jnp.zeros((pad_rows, width_x), jnp.float32))
         stacked = jnp.concatenate(split_three(jnp.concatenate(parts, axis=0)), axis=0)
-        return dot(t_tall[...], stacked) * STENCIL_SCALE
+        return dot(t_tall[:, :tall], stacked) * STENCIL_SCALE
 
     def slope_x(field):
         value = field.reshape(group * rows, width_x)
-        return (dot_exact(value, t_wide[...]) * STENCIL_SCALE).reshape(group, rows, width_x)
+        return (dot_exact(value, t_wide) * STENCIL_SCALE).reshape(group, rows, width_x)
 
     for spin in range(2):
         grad_x[spin] = slope_x(main[spin, REACH : REACH + group])
 
     def gradients(plane, carry):
         for spin in range(2):
+            grad_y[spin, plane] = slope_y(main[spin, REACH + plane], halo_in[plane, spin])
+        return carry
+
+    lax.fori_loop(0, group, gradients, 0)
+    def near_wait(first):
+        def body(step, carry):
+            main_copy(member, me, first + step, 1).wait_recv()
+            return carry
+
+        lax.fori_loop(0, REACH, body, 0)
+
+    @pl.when(level > 0)
+    def _():
+        near_wait(0)
+
+    @pl.when(level < levels - 1)
+    def _():
+        near_wait(REACH + group)
+
+
+    def gradients_z(plane, carry):
+        for spin in range(2):
             grad_z[spin, plane] = slope_z(main, spin, plane)
-            grad_y[spin, plane] = slope_y(main[spin, REACH + plane], halo_in[plane, spin])
-        return carry
-
-    lax.fori_loop(0, group, gradients, 0)
+        return carry
+
+    lax.fori_loop(0, group, gradients_z, 0)
 
     chunk = SUBLANES
 
@@ -650,11 +700,31 @@
     def _():
         flux_y_copy(1, me - 1).start()
 
-    around(lambda step, peer, origin: spec_copy(step, peer, origin).wait_recv())
+    @pl.when(me == first_device)
+    def _():
+        remote(edge_out, edge_in, edge_s, edge_r, edge_device).wait_recv()
+        edge_out[:, :width_x] = edge_in[:, :width_x]
+        edge_out[:, width_x:] = dot_exact(edge_in[:, width_x:], t_turn)
+        top = lax.broadcasted_iota(jnp.int32, (slots, LANES), 0) == 0
+
+        def mix(kz, carry):
+            other = edge_out[pl.ds(kz, 1), :]
+            for t in range(2 * tiles):
+                mine = k_self[kz, t]
+                theirs = other[:, t * LANES : (t + 1) * LANES]
+                k_self[kz, t] = jnp.where(top, 0.5 * (mine + theirs), mine)
+                k_cross[kz, t] = jnp.where(top, 0.5 * (mine - theirs), 0.0)
+            return carry
+
+        lax.fori_loop(0, planes_k, mix, 0)
+
+    loads[4].wait()
+    others = pl.ds(0, devices - 1)
+    remote(spec_out.at[others], spec_in.at[others], spec_s, spec_r, me).wait_recv()
     lane = lax.broadcasted_iota(jnp.int32, (1, 1, width_x), 2)
     first = lane == 0
     high, low = split(spec_in[...].reshape(depth * 2 * slots, width_x))
-    wide = dot(high, tx_high[...]) + (dot(low, tx_high[...]) + dot(high, tx_low[...]))
+    wide = jnp.concatenate(from_right(5, high, low), axis=1)
     wide = wide.reshape(depth, 2, slots, 2 * width_x)
     cos_re, cos_im = wide[:, 0, :, :width_x], wide[:, 1, :, :width_x]
     sin_re, sin_im = wide[:, 0, :, width_x:], wide[:, 1, :, width_x:]
@@ -730,12 +800,11 @@
         x_in[:, 0, :, there] = jnp.where(keep, minus_re, minus_im - plus_im)
         x_in[:, 1, :, there] = jnp.where(keep, minus_im, plus_re - minus_re)
     high, low = split(x_in[...].reshape(depth * 2 * slots, 2 * width_x))
-    values = dot(high, tr_high[...]) + (dot(low, tr_high[...]) + dot(high, tr_low[...]))
-    back_out[...] = values.reshape(back_out.shape)
+    back_out[...] = jnp.concatenate(from_right(7, high, low), axis=1).reshape(back_out.shape)
 
     def back_copy(step, peer, slot):
         return remote(
-            back_out.at[peer], back_in.at[slot], back_s.at[step], back_r.at[step], peer
+            back_out.at[peer], back_in.at[slot], back_s, back_r, peer
         )
 
     around(lambda step, peer, origin: back_copy(step, peer, me).start())
@@ -745,11 +814,11 @@
     row = lax.broadcasted_iota(jnp.int32, acc.shape, 0)
     single = jnp.logical_and(me == first_device, lax.rem(row, slots) == 0)
     energy_h = jnp.sum(jnp.where(single, acc, 2.0 * acc)) * (0.5 / (8.0 * cells) / cells)
-    row = lax.broadcasted_iota(jnp.int32, partial.shape, 0)
-    partial[...] = jnp.where(row == 0, energy_xc, energy_h)
+    lane = lax.broadcasted_iota(jnp.int32, partial.shape, 1)
+    partial[...] = jnp.where(lane == 0, energy_xc, energy_h)
 
     def part_copy(step, peer, slot):
-        return remote(partial, sums.at[slot], part_s.at[step], part_r.at[step], peer)
+        return remote(partial, sums.at[slot], part_s, part_r, peer)
 
     around(lambda step, peer, origin: part_copy(step, peer, me).start())
     sums[me] = partial[...]
@@ -793,37 +862,35 @@
 
     def v_copy(b, peer, source):
         return remote(
-            v_own.at[:, b], v_all.at[:, block(source)], v_s.at[b], v_r.at[source], peer
+            v_own.at[:, b], v_all.at[:, block(source)], v_s, v_r, peer
         )
 
     in_group(lambda b, peer: v_copy(b, peer, member).start())
     v_all[:, block(member)] = v_own[:, member]
 
-    locals_[1].wait()
-    locals_[2].wait()
-    around(lambda step, peer, origin: back_copy(step, peer, origin).wait_recv())
+    remote(back_out.at[others], back_in.at[others], back_s, back_r, me).wait_recv()
     high, low = split(back_in[...].reshape(depth * 2 * slots, width_x))
-    hartree = dot(tb_high[...], high) + (dot(tb_high[...], low) + dot(tb_low[...], high))
-    in_group(lambda b, peer: v_copy(b, peer, b).wait_recv())
-    out[0] = hartree + v_all[0]
-    out[1] = hartree + v_all[1]
-    around(lambda step, peer, origin: part_copy(step, peer, origin).wait_recv())
-    e_out[...] = jnp.sum(sums[...], axis=0)
-
-    def sent(b, peer):
-        main_copy(b, peer, REACH + member, 0).wait_send()
-        halo_copy(b, peer, member).wait_send()
-        v_copy(b, peer, member).wait_send()
-
-    in_group(sent)
-    near_each(lambda copy: copy.wait_send())
-
-    def sent_around(step, peer, origin):
-        spec_copy(step, peer, me).wait_send()
-        back_copy(step, peer, me).wait_send()
-        part_copy(step, peer, me).wait_send()
-
-    around(sent_around)
+    hartree[...] = from_left(9, high, low)
+    remote(v_own.at[:, mates], v_own.at[:, mates], v_s, v_r, me).wait_recv()
+    remote(sums.at[others], sums.at[others], part_s, part_r, me).wait_recv()
+
+    seven = main.at[:, mates]
+    remote(seven, seven, main_s.at[0], main_r.at[0], me).wait_send()
+    remote(halo_out.at[mates], halo_in.at[mates], halo_s, halo_r, me).wait_send()
+    remote(seven, seven, v_s, v_r, me).wait_send()
+    four = main.at[:, pl.ds(0, REACH)]
+
+    @pl.when(has_near)
+    def _():
+        remote(four, four, main_s.at[1], main_r.at[0], me).wait_send()
+
+    @pl.when(has_relay)
+    def _():
+        remote(four, four, relay_s, main_r.at[0], me).wait_send()
+
+    remote(spec_out.at[others], spec_in.at[others], spec_s, spec_r, me).wait_send()
+    remote(back_out.at[others], back_in.at[others], back_s, back_r, me).wait_send()
+    remote(sums.at[others], sums.at[others], part_s, part_r, me).wait_send()
 
     @pl.when(exists_up)
     def _():
@@ -844,6 +911,15 @@
     @pl.when(me == edge_device)
     def _():
         remote(edge_out, edge_in, edge_s, edge_r, first_device).wait_send()
+
+
+def join_kernel(hartree, v_all, sums, out, energies):
+    out[0] = hartree[...] + v_all[0]
+    out[1] = hartree[...] + v_all[1]
+    both = jnp.sum(sums[...], axis=0)
+    lane = lax.broadcasted_iota(jnp.int32, both.shape, 1)
+    energies[0] = jnp.sum(jnp.where(lane == 0, both, 0.0))
+    energies[1] = jnp.sum(jnp.where(lane == 1, both, 0.0))
 
 
 def per_device(density, kernel_hat):
@@ -860,17 +936,25 @@
     full = 2 * devices
     n1 = 1 << (full.bit_length() // 2)
     ty_high, ty_low, tb_high, tb_low = y_tables(width_y, devices, 1.0 / (8 * cells))
-    x_parts = x_tables(width_x)
-    t_wide, t_tall = slope_tables(width_x, rows)
+    tables = (
+        ty_high,
+        ty_low,
+        turn_table(width_x),
+        *slope_tables(width_x, rows),
+        *x_tables(width_x),
+        tb_high,
+        tb_low,
+    )
+    packed, places = pack(tables)
     spec_shape = (devices, 2 * slots, width_x)
     tile_shape = (2, group, rows, width_x)
     tall_shape = (2, group + 2 * REACH, rows, width_x)
     f32 = functools.partial(pltpu.VMEM, dtype=jnp.float32)
     dma = pltpu.SemaphoreType.DMA
     scratch = [
+        f32((2, width_y, width_x)),
         f32(kernel_hat.shape),
-        pltpu.VMEM(tb_high.shape, jnp.bfloat16),
-        pltpu.VMEM(tb_low.shape, jnp.bfloat16),
+        pltpu.VMEM(packed.shape, packed.dtype),
         f32(spec_shape),
         f32(spec_shape),
         f32((group, 2, SUBLANES, width_x)),
@@ -883,7 +967,6 @@
         f32((group, 2, SUBLANES, width_x)),
         f32((2, group, 2, SUBLANES, width_x)),
         f32(tile_shape),
-        f32((2, width_y, width_x)),
         f32((full, 2 * width_x)),
         f32((full, 2 * width_x)),
         f32((full, slots, width_x)),
@@ -895,54 +978,44 @@
         f32((devices, 2, slots, 2 * width_x)),
         f32(spec_shape),
         f32(spec_shape),
-        f32((SUBLANES, LANES)),
-        f32((devices, SUBLANES, LANES)),
-        dma((3,)),
-        dma((devices,)),
-        dma((devices,)),
-        dma((devices,)),
-        dma((devices,)),
-        dma((devices,)),
-        dma((devices,)),
-        dma((2, group)),
+        f32((1, LANES)),
+        dma((5,)),
+        *[dma] * 6,
+        dma((2,)),
         dma((group + 2 * REACH,)),
-        dma((group,)),
-        dma((group,)),
-        dma((2,)),
-        dma((2,)),
-        dma((2,)),
-        dma((2,)),
-        dma((group,)),
-        dma((group,)),
-        dma,
-        dma,
+        *[dma] * 3,
+        *[dma((2,))] * 4,
+        *[dma] * 4,
     ]
+    held = sum(math.prod(part.shape) for part in scratch if hasattr(part, "memory_space"))
+    limit = max(VMEM_BYTES, min(VMEM_MOST, 8 * held))
+    pieces = pl.pallas_call(
+        functools.partial(mega_kernel, devices, group, half, places),
+        out_shape=(
+            jax.ShapeDtypeStruct((width_y, width_x), jnp.float32),
+            jax.ShapeDtypeStruct((2, width_y, width_x), jnp.float32),
+            jax.ShapeDtypeStruct((devices, 1, LANES), jnp.float32),
+        ),
+        in_specs=[HBM_SPEC] * 3,
+        out_specs=(VMEM_SPEC,) * 3,
+        scratch_shapes=scratch,
+        compiler_params=pltpu.CompilerParams(
+            collective_id=0, has_side_effects=True, vmem_limit_bytes=limit
+        ),
+        name="potential",
+    )(density.reshape(2, width_y, width_x), kernel_hat, packed)
     potential, energies = pl.pallas_call(
-        functools.partial(mega_kernel, devices, group, half),
+        join_kernel,
         out_shape=(
             jax.ShapeDtypeStruct((2, width_y, width_x), jnp.float32),
-            jax.ShapeDtypeStruct((SUBLANES, LANES), jnp.float32),
+            jax.ShapeDtypeStruct((2,), jnp.float32),
         ),
-        in_specs=[VMEM_SPEC] * 3 + [ANY_SPEC] * 3 + [VMEM_SPEC] * 7,
-        out_specs=(VMEM_SPEC, VMEM_SPEC),
-        scratch_shapes=scratch,
-        compiler_params=pltpu.CompilerParams(
-            collective_id=0, has_side_effects=True, vmem_limit_bytes=VMEM_BYTES
-        ),
-        name="potential",
-    )(
-        density.reshape(2, width_y, width_x),
-        ty_high,
-        ty_low,
-        kernel_hat,
-        tb_high,
-        tb_low,
-        *x_parts,
-        t_wide,
-        t_tall,
-        turn_table(width_x),
-    )
-    return potential.reshape(density.shape), energies[:2, 0]
+        in_specs=[VMEM_SPEC] * 3,
+        out_specs=(VMEM_SPEC, pl.BlockSpec(memory_space=pltpu.SMEM)),
+        compiler_params=pltpu.CompilerParams(vmem_limit_bytes=8 << 20),
+        name="join",
+    )(*pieces)
+    return potential.reshape(density.shape), energies
 
 
 def solution(mesh):

time: 63.1 us -> 50.3 us (0.80)
  Pallas kernels: 59 us -> 48.4 us
  local copies, waits for them, and re-layouts: 3.18 us -> 1.03 us
    pallas_call x1 -> x2, Pallas kernels: 59 us -> 48.4 us  [the longest x1 47.5 us: per_device(): pl.pallas_call(functools.partial(mega_kernel, devices, group, half, place...]
    slice x1 -> x0, local copies, waits for them, and re-layouts: 1.31 us -> none  [per_device(): return (potential.reshape(density.shape), energies[:2, 0])]
    unnamed x1 -> x2, local copies, waits for them, and re-layouts: 1.87 us -> 1.03 us
where the time goes in v2:
time: 50.3 us; the launch traced here: 50 us
  Pallas kernels  48.4 us (96%)
  local copies, waits for them, and re-layouts  1.03 us (2%)
  between operations  0.65 us (1%)
    pallas_call x1, Pallas kernels, per_device(): pl.pallas_call(functools.partial(mega_kernel, devices, group, half, place...  47.5 us
    unnamed x2, local copies, waits for them, and re-layouts  1.03 us

profile of v2, /device:TPU:0, one launch (start us, length us, event | category | flops | bytes accessed | tf_op | source)
XLA Modules:
  0.0 50.0 jit_solution(7038911960558548383)
XLA Ops:
  0.6 0.0 copy-start
  0.6 1.0 %copy-done = f32[2,1,256,256]{3,2,1,0:T(8,128)S(1)} copy-done((f32[2,1,256,256]{3,2,1,0:T(8,128)S(1)}, f32[2,1,256,256]{3,2,1,0:T(8,128)}, u32[]{:S(2)}) %copy-start) | copy-done | bytes 524312
  1.7 47.5 %potential.1 = (f32[256,256]{1,0:T(8,128)S(1)}, f32[2,256,256]{2,1,0:T(8,128)S(1)}, f32[32,1,128]{2,1,0:T(1,128)S(1)}) custom-call(f32[2,256,256]{2,1,0:T(8,128)S(1)} %bitcast.4, f32[64,16,512]{2,1,0:T(8,128)} %refs_1_.1, bf16[4640,256]{1,0:T(8,128)(2,1)} %constant.2.clone.refs_2_), custom_call_target="tpu_custom_call" | custom-call | tf_op jit(solution)/shard_map/potential/pallas_call | solution.py:992
  49.2 0.9 %join.1 = (f32[2,256,256]{2,1,0:T(8,128)}, f32[2]{0:T(128)}) custom-call(f32[256,256]{1,0:T(8,128)S(1)} %get-tuple-element.7.hartree, f32[2,256,256]{2,1,0:T(8,128)S(1)} %get-tuple-element.8.v_all, f32[32,1,128]{2,1,0:T(1,128)S(1)} %get-tuple-element.9.sums), custom_call_target="tpu_custom_call" | custom-call | tf_op jit(solution)/shard_map/join/pallas_call | solution.py:1007
Async XLA Ops:
  0.6 1.0 %copy-start = (f32[2,1,256,256]{3,2,1,0:T(8,128)S(1)}, f32[2,1,256,256]{3,2,1,0:T(8,128)}, u32[]{:S(2)}) copy-start(f32[2,1,256,256]{3,2,1,0:T(8,128)} %param.3) | copy-start | bytes 1572868

commit v3 on v2

--- a/solution.py
+++ b/solution.py
@@ -28,9 +28,9 @@
 PACK = 256
 VMEM_SPEC = pl.BlockSpec(memory_space=pltpu.VMEM)
 HBM_SPEC = pl.BlockSpec(memory_space=pltpu.HBM)
-VMEM_BYTES = 52 * 1024 * 1024
+VMEM_BYTES = 53 * 1024 * 1024
 VMEM_MOST = 63 * 1024 * 1024
-EARLY = 8
+EARLY = 12
 
 
 def exchange_spin(dens, log_dens, sigma):
@@ -352,6 +352,7 @@
     first_device, edge_device = 0, devices // 2
     cells = depth * width_y * width_x
 
+
     barrier = pltpu.get_barrier_semaphore()
 
     def greet(step, carry):
@@ -403,6 +404,7 @@
             device_id_type=MESH,
         )
 
+
     loads[0].wait()
     sub_row = lax.broadcasted_iota(jnp.int32, (1, SUBLANES, width_x), 1)
     for b in range(group):
@@ -410,7 +412,9 @@
         below = dens[:, b * rows - SUBLANES : b * rows] if b else 0.0
         halo_out[b] = jnp.where(sub_row < REACH, above, below)
 
+
     pl.semaphore_wait(barrier, devices - 1)
+
 
     upper = member >= REACH
     own_half = jnp.where(upper, REACH, 0)
@@ -483,9 +487,11 @@
     lax.fori_loop(0, REACH, start_far, 0)
     lax.fori_loop(1, REACH, start_own, 0)
 
+
     loads[1].wait()
     high, low = split(dens[0] + dens[1])
     spec_out[...] = from_left(0, high, low).reshape(spec_out.shape)
+
     loads[2].wait()
 
     @pl.when(me == edge_device)
@@ -493,24 +499,30 @@
         edge_out[...] = khat[:, 0, :]
         remote(edge_out, edge_in, edge_s, edge_r, first_device).start()
 
-    def spec_copy(step, peer, slot):
+    def spec_copy(peer, slot):
         return remote(
             spec_out.at[peer], spec_in.at[slot], spec_s, spec_r, peer
         )
 
-    def around(act, first=1, last=devices):
+    crossing = group * (levels - 1)
+
+    def around(act, first=0, last=devices - 1):
         def body(index, carry):
-            away = lax.div(index, 2)
-            step = devices // 2 + jnp.where(lax.rem(index, 2) == 0, away, -away)
-            act(step, lax.rem(me + step, devices), lax.rem(me - step + devices, devices))
+            inner = index >= crossing
+            away = lax.rem(lax.div(index, group), levels - 1)
+            hop = lax.div(away + 1, 2)
+            hop = levels // 2 + jnp.where(lax.rem(away, 2) == 0, hop, -hop)
+            turn_by = jnp.where(inner, index - crossing + 1, lax.rem(index, group))
+            hop = jnp.where(inner, 0, hop)
+            act(lax.rem(level + hop, levels) * group + lax.rem(member + turn_by, group))
             return carry
 
         lax.fori_loop(first, last, body, 0)
 
-    def start_spec(step, peer, origin):
-        spec_copy(step, peer, me).start()
-
-    around(start_spec, last=1 + EARLY)
+    def start_spec(peer):
+        spec_copy(peer, me).start()
+
+    around(start_spec, last=EARLY)
     main[:, REACH + member] = dens[:, block(member)]
     halo_in[member] = halo_out[member]
     spec_in[me] = spec_out[me]
@@ -526,6 +538,7 @@
     def _():
         main[:, REACH + group :] = zero_planes
         flux_z[:, REACH + group :] = zero_planes
+
 
     loads[3].wait()
     (t_turn,), (t_wide,), (t_tall,) = blocks(2), blocks(3), blocks(4)
@@ -556,6 +569,7 @@
 
     lax.fori_loop(0, planes_k, clear, 0)
 
+
     def finish_main(b, peer):
         main_copy(b, peer, REACH + b, 0).wait_recv()
 
@@ -570,7 +584,7 @@
         return carry
 
     lax.fori_loop(0, REACH, finish_far, 0)
-    around(start_spec, first=1 + EARLY)
+    around(start_spec, first=EARLY)
 
     def finish_own(step, carry):
         b = own_half + lax.rem(member + step, REACH)
@@ -580,6 +594,7 @@
     lax.fori_loop(1, REACH, finish_own, 0)
     mates = pl.ds(0, group - 1)
     remote(halo_out.at[mates], halo_in.at[mates], halo_s, halo_r, me).wait_recv()
+
 
     def slope_z(field, spin, plane):
         result = 0.0
@@ -612,6 +627,7 @@
         return carry
 
     lax.fori_loop(0, group, gradients, 0)
+
     def near_wait(first):
         def body(step, carry):
             main_copy(member, me, first + step, 1).wait_recv()
@@ -634,6 +650,7 @@
         return carry
 
     lax.fori_loop(0, group, gradients_z, 0)
+
 
     chunk = SUBLANES
 
@@ -661,11 +678,6 @@
         grad_x[1, plane, at] = d_dd * dx + d_ud * ux
         return acc + energy
 
-    energy_acc = lax.fori_loop(
-        0, group * rows // chunk, point, jnp.zeros((chunk, width_x), jnp.float32)
-    )
-    energy_xc = jnp.sum(energy_acc) * (1.0 / cells)
-
     def flux_z_copy(side, peer):
         source = (slice(group, group + REACH), slice(REACH, 2 * REACH))[side]
         target = (slice(0, REACH), slice(REACH + group, 2 * REACH + group))[side]
@@ -679,13 +691,21 @@
     exists_up, exists_down = level < levels - 1, level > 0
     right, left = member < group - 1, member > 0
 
+    steps = group * rows // chunk
+    energy_acc = jnp.zeros((chunk, width_x), jnp.float32)
+    energy_acc = lax.fori_loop(steps // 2, steps, point, energy_acc)
+
     @pl.when(exists_up)
     def _():
         flux_z_copy(0, me + group).start()
 
+    energy_acc = lax.fori_loop(0, steps // 2, point, energy_acc)
+
     @pl.when(exists_down)
     def _():
         flux_z_copy(1, me - group).start()
+
+    energy_xc = jnp.sum(energy_acc) * (1.0 / cells)
 
     for spin in range(2):
         flux_out[:, spin] = jnp.where(
@@ -699,6 +719,7 @@
     @pl.when(left)
     def _():
         flux_y_copy(1, me - 1).start()
+
 
     @pl.when(me == first_device)
     def _():
@@ -718,9 +739,15 @@
 
         lax.fori_loop(0, planes_k, mix, 0)
 
+
+    for spin in range(2):
+        v_own[spin] = v_own[spin] - slope_x(grad_x[spin])
+
+
     loads[4].wait()
     others = pl.ds(0, devices - 1)
     remote(spec_out.at[others], spec_in.at[others], spec_s, spec_r, me).wait_recv()
+
     lane = lax.broadcasted_iota(jnp.int32, (1, 1, width_x), 2)
     first = lane == 0
     high, low = split(spec_in[...].reshape(depth * 2 * slots, width_x))
@@ -739,6 +766,7 @@
                     :, :, t * LANES : (t + 1) * LANES
                 ]
 
+
     n1, n2 = z_mid.shape[:2]
     full = n1 * n2
 
@@ -760,6 +788,7 @@
         return carry
 
     lax.fori_loop(0, 2 * tiles, fore, 0)
+
     lane = lax.broadcasted_iota(jnp.int32, (slots, LANES), 1)
 
     def back(col, carry):
@@ -789,6 +818,7 @@
         return carry
 
     lax.fori_loop(0, 2 * tiles, back, 0)
+
     for t in range(tiles):
         keep = lax.broadcasted_iota(jnp.int32, (1, 1, LANES), 2) + t * LANES == 0
         plus_re, plus_im = z_in[:, 0, t], z_in[:, 1, t]
@@ -802,13 +832,67 @@
     high, low = split(x_in[...].reshape(depth * 2 * slots, 2 * width_x))
     back_out[...] = jnp.concatenate(from_right(7, high, low), axis=1).reshape(back_out.shape)
 
-    def back_copy(step, peer, slot):
+
+    def back_copy(peer, slot):
         return remote(
             back_out.at[peer], back_in.at[slot], back_s, back_r, peer
         )
 
-    around(lambda step, peer, origin: back_copy(step, peer, me).start())
+    around(lambda peer: back_copy(peer, me).start(), first=crossing)
+    around(lambda peer: back_copy(peer, me).start(), last=crossing)
     back_in[me] = back_out[me]
+
+
+    @pl.when(left)
+    def _():
+        flux_y_copy(0, me).wait_recv()
+
+    @pl.when(right)
+    def _():
+        flux_y_copy(1, me).wait_recv()
+
+    @pl.when(jnp.logical_not(left))
+    def _():
+        flux_in[0] = jnp.zeros(flux_in.shape[1:], jnp.float32)
+
+    @pl.when(jnp.logical_not(right))
+    def _():
+        flux_in[1] = jnp.zeros(flux_in.shape[1:], jnp.float32)
+
+
+    def divergence(plane, carry):
+        for spin in range(2):
+            outer = jnp.where(sub_row[0] < REACH, flux_in[1, plane, spin], flux_in[0, plane, spin])
+            v_own[spin, plane] = v_own[spin, plane] - slope_y(grad_y[spin, plane], outer)
+        return carry
+
+    lax.fori_loop(0, group, divergence, 0)
+
+
+    @pl.when(exists_down)
+    def _():
+        flux_z_copy(0, me).wait_recv()
+
+    @pl.when(exists_up)
+    def _():
+        flux_z_copy(1, me).wait_recv()
+
+
+    def divergence_z(plane, carry):
+        for spin in range(2):
+            v_own[spin, plane] = v_own[spin, plane] - slope_z(flux_z, spin, plane)
+        return carry
+
+    lax.fori_loop(0, group, divergence_z, 0)
+
+    def v_copy(b, peer, source):
+        return remote(
+            v_own.at[:, b], v_all.at[:, block(source)], v_s, v_r, peer
+        )
+
+    in_group(lambda b, peer: v_copy(b, peer, member).start())
+    v_all[:, block(member)] = v_own[:, member]
+
 
     acc = jnp.sum(spec_in[...] * back_out[...], axis=0)
     row = lax.broadcasted_iota(jnp.int32, acc.shape, 0)
@@ -817,62 +901,22 @@
     lane = lax.broadcasted_iota(jnp.int32, partial.shape, 1)
     partial[...] = jnp.where(lane == 0, energy_xc, energy_h)
 
-    def part_copy(step, peer, slot):
+    def part_copy(peer, slot):
         return remote(partial, sums.at[slot], part_s, part_r, peer)
 
-    around(lambda step, peer, origin: part_copy(step, peer, me).start())
+    around(lambda peer: part_copy(peer, me).start())
     sums[me] = partial[...]
 
-    @pl.when(exists_down)
-    def _():
-        flux_z_copy(0, me).wait_recv()
-
-    @pl.when(exists_up)
-    def _():
-        flux_z_copy(1, me).wait_recv()
-
-    @pl.when(left)
-    def _():
-        flux_y_copy(0, me).wait_recv()
-
-    @pl.when(right)
-    def _():
-        flux_y_copy(1, me).wait_recv()
-
-    @pl.when(jnp.logical_not(left))
-    def _():
-        flux_in[0] = jnp.zeros(flux_in.shape[1:], jnp.float32)
-
-    @pl.when(jnp.logical_not(right))
-    def _():
-        flux_in[1] = jnp.zeros(flux_in.shape[1:], jnp.float32)
-
-    for spin in range(2):
-        v_own[spin] = v_own[spin] - slope_x(grad_x[spin])
-
-    def divergence(plane, carry):
-        for spin in range(2):
-            outer = jnp.where(sub_row[0] < REACH, flux_in[1, plane, spin], flux_in[0, plane, spin])
-            v_own[spin, plane] = v_own[spin, plane] - (
-                slope_z(flux_z, spin, plane) + slope_y(grad_y[spin, plane], outer)
-            )
-        return carry
-
-    lax.fori_loop(0, group, divergence, 0)
-
-    def v_copy(b, peer, source):
-        return remote(
-            v_own.at[:, b], v_all.at[:, block(source)], v_s, v_r, peer
-        )
-
-    in_group(lambda b, peer: v_copy(b, peer, member).start())
-    v_all[:, block(member)] = v_own[:, member]
 
     remote(back_out.at[others], back_in.at[others], back_s, back_r, me).wait_recv()
+
     high, low = split(back_in[...].reshape(depth * 2 * slots, width_x))
     hartree[...] = from_left(9, high, low)
+
     remote(v_own.at[:, mates], v_own.at[:, mates], v_s, v_r, me).wait_recv()
+
     remote(sums.at[others], sums.at[others], part_s, part_r, me).wait_recv()
+
 
     seven = main.at[:, mates]
     remote(seven, seven, main_s.at[0], main_r.at[0], me).wait_send()

time: 50.3 us -> 48.8 us (0.970)
  local copies, waits for them, and re-layouts: 1.03 us -> 0 us
    unnamed x2 -> x0, local copies, waits for them, and re-layouts: 1.03 us -> none
where the time goes in v3:
time: 48.8 us; the launch traced here: 48.6 us
  Pallas kernels  48 us (98%)
  between operations  0.64 us (1%)
    pallas_call x1, Pallas kernels, per_device(): pl.pallas_call(functools.partial(mega_kernel, devices, group, half, place...  47.1 us

profile of v3, /device:TPU:0, one launch (start us, length us, event | category | flops | bytes accessed | tf_op | source)
XLA Modules:
  0.0 48.6 jit_solution(13317895481968914832)
XLA Ops:
  0.6 47.1 %potential.1 = (f32[256,256]{1,0:T(8,128)S(1)}, f32[2,256,256]{2,1,0:T(8,128)S(1)}, f32[32,1,128]{2,1,0:T(1,128)S(1)}) custom-call(f32[2,256,256]{2,1,0:T(8,128)} %bitcast.4, f32[64,16,512]{2,1,0:T(8,128)} %refs_1_.1, bf16[4640,256]{1,0:T(8,128)(2,1)} %constant.2.clone.refs_2_), custom_call_target="tpu_custom_call" | custom-call | tf_op jit(solution)/shard_map/potential/pallas_call | solution.py:1036
  47.8 0.9 %join.1 = (f32[2,256,256]{2,1,0:T(8,128)}, f32[2]{0:T(128)}) custom-call(f32[256,256]{1,0:T(8,128)S(1)} %get-tuple-element.7.hartree, f32[2,256,256]{2,1,0:T(8,128)S(1)} %get-tuple-element.8.v_all, f32[32,1,128]{2,1,0:T(1,128)S(1)} %get-tuple-element.9.sums), custom_call_target="tpu_custom_call" | custom-call | tf_op jit(solution)/shard_map/join/pallas_call | solution.py:1051

commit v4 on v3

--- a/solution.py
+++ b/solution.py
@@ -31,13 +31,12 @@
 VMEM_BYTES = 53 * 1024 * 1024
 VMEM_MOST = 63 * 1024 * 1024
 EARLY = 12
-
-
-def exchange_spin(dens, log_dens, sigma):
+KNOWN = 11
+
+
+def exchange_spin(dens, cube, sigma):
     factor = -0.75 * (3.0 / math.pi) ** (1.0 / 3.0) * 2.0 ** (1.0 / 3.0)
     scale = (3.0 * math.pi**2) ** (2.0 / 3.0) * 2.0 ** (8.0 / 3.0)
-    inverse_cube = jnp.exp(log_dens * (-1.0 / 3.0))
-    cube = dens * inverse_cube * inverse_cube
     product = dens * cube
     weight = product * product
     bent = (MU_X / (KAPPA * scale)) * sigma
@@ -49,7 +48,7 @@
     by_dens = factor * cube * ((4.0 / 3.0) * enhance - (8.0 / 3.0) * rest * share)
     square = dens * dens * inverse
     by_sigma = (factor * MU_X / scale) * square * square
-    return energy, by_dens, by_sigma, cube, inverse_cube
+    return energy, by_dens, by_sigma
 
 
 def pw_piece(root, square, params):
@@ -68,9 +67,11 @@
     return value, by_root
 
 
-def xc_point(up, down, sigma_uu, sigma_ud, sigma_dd):
-    energy_u, vx_u, by_uu, cube_u, inverse_u = exchange_spin(up, jnp.log(up), sigma_uu)
-    energy_d, vx_d, by_dd, cube_d, inverse_d = exchange_spin(down, jnp.log(down), sigma_dd)
+def xc_density(up, down):
+    inverse_u = jnp.exp(jnp.log(up) * (-1.0 / 3.0))
+    inverse_d = jnp.exp(jnp.log(down) * (-1.0 / 3.0))
+    cube_u = up * inverse_u * inverse_u
+    cube_d = down * inverse_d * inverse_d
     total = up + down
     sixth = jnp.exp(jnp.log(total) * (-1.0 / 6.0))
     inverse_cube = sixth * sixth
@@ -113,6 +114,20 @@
     weight_a = ratio / (jnp.exp(expo) - 1.0)
     scale = math.pi / (16.0 * (3.0 * math.pi**2) ** (1.0 / 3.0))
     to_t = scale * phi_square * (inverse_square * inverse_cube) * (inverse_square * inverse_square)
+    slope = (1.0 / 6.0) * root * local_root
+    return (
+        cube_u, cube_d, zeta, local, slope, local_zeta, by_phi, inverse_phi, gamma_phi, weight_a, to_t
+    )
+
+
+def xc_gradient(up, down, given, sigma_uu, sigma_ud, sigma_dd):
+    cube_u, cube_d, zeta, local, slope, local_zeta, by_phi, inverse_phi, gamma_phi, weight_a, to_t = given
+    energy_u, vx_u, by_uu = exchange_spin(up, cube_u, sigma_uu)
+    energy_d, vx_d, by_dd = exchange_spin(down, cube_d, sigma_dd)
+    total = up + down
+    ratio = BETA_C / GAMMA_C
+    inverse_gamma = inverse_phi * inverse_phi * inverse_phi * (1.0 / GAMMA_C)
+    expo = -local * inverse_gamma
     sigma = sigma_uu + 2.0 * sigma_ud + sigma_dd
     tee = sigma * to_t
     why = weight_a * tee
@@ -130,14 +145,14 @@
     tee_part = tee * by_tee
     phi_part = (3.0 * gradient - 3.0 * expo * chain - 2.0 * tee_part) * inverse_phi
     corr = local + gradient
-    by_total = corr - (1.0 / 6.0) * root * local_root * by_local - (7.0 / 3.0) * tee_part
+    by_total = corr - slope * by_local - (7.0 / 3.0) * tee_part
     by_zeta = by_local * local_zeta + phi_part * by_phi
     by_sigma = total * by_tee * to_t
     energy = energy_u + energy_d + total * corr
     return (
         energy,
-        vx_u + by_total + by_zeta * minus,
-        vx_d + by_total - by_zeta * plus,
+        vx_u + by_total + by_zeta * (1.0 - zeta),
+        vx_d + by_total - by_zeta * (1.0 + zeta),
         by_uu + by_sigma,
         2.0 * by_sigma,
         by_dd + by_sigma,
@@ -303,6 +318,7 @@
         grad_x,
         grad_y,
         grad_z,
+        known,
         flux_z,
         flux_out,
         flux_in,
@@ -352,7 +368,6 @@
     first_device, edge_device = 0, devices // 2
     cells = depth * width_y * width_x
 
-
     barrier = pltpu.get_barrier_semaphore()
 
     def greet(step, carry):
@@ -404,7 +419,6 @@
             device_id_type=MESH,
         )
 
-
     loads[0].wait()
     sub_row = lax.broadcasted_iota(jnp.int32, (1, SUBLANES, width_x), 1)
     for b in range(group):
@@ -412,9 +426,7 @@
         below = dens[:, b * rows - SUBLANES : b * rows] if b else 0.0
         halo_out[b] = jnp.where(sub_row < REACH, above, below)
 
-
     pl.semaphore_wait(barrier, devices - 1)
-
 
     upper = member >= REACH
     own_half = jnp.where(upper, REACH, 0)
@@ -487,11 +499,9 @@
     lax.fori_loop(0, REACH, start_far, 0)
     lax.fori_loop(1, REACH, start_own, 0)
 
-
     loads[1].wait()
     high, low = split(dens[0] + dens[1])
     spec_out[...] = from_left(0, high, low).reshape(spec_out.shape)
-
     loads[2].wait()
 
     @pl.when(me == edge_device)
@@ -539,7 +549,6 @@
         main[:, REACH + group :] = zero_planes
         flux_z[:, REACH + group :] = zero_planes
 
-
     loads[3].wait()
     (t_turn,), (t_wide,), (t_tall,) = blocks(2), blocks(3), blocks(4)
     lower = me < edge_device
@@ -569,7 +578,6 @@
 
     lax.fori_loop(0, planes_k, clear, 0)
 
-
     def finish_main(b, peer):
         main_copy(b, peer, REACH + b, 0).wait_recv()
 
@@ -585,16 +593,34 @@
 
     lax.fori_loop(0, REACH, finish_far, 0)
     around(start_spec, first=EARLY)
+    chunk = 2 * SUBLANES
+
+    def density_part(plane):
+        def body(index, carry):
+            at = pl.ds(pl.multiple_of(index * chunk, chunk), chunk)
+            parts = xc_density(main[0, REACH + plane, at], main[1, REACH + plane, at])
+            for i, part in enumerate(parts):
+                known[i, plane, at] = part
+            return carry
+
+        lax.fori_loop(0, rows // chunk, body, 0)
+
+    def density_far(step, carry):
+        density_part(far_half + step)
+        return carry
+
+    density_part(member)
+    lax.fori_loop(0, REACH, density_far, 0)
 
     def finish_own(step, carry):
         b = own_half + lax.rem(member + step, REACH)
         finish_main(b, base + b)
+        density_part(b)
         return carry
 
     lax.fori_loop(1, REACH, finish_own, 0)
     mates = pl.ds(0, group - 1)
     remote(halo_out.at[mates], halo_in.at[mates], halo_s, halo_r, me).wait_recv()
-
 
     def slope_z(field, spin, plane):
         result = 0.0
@@ -627,7 +653,6 @@
         return carry
 
     lax.fori_loop(0, group, gradients, 0)
-
     def near_wait(first):
         def body(step, carry):
             main_copy(member, me, first + step, 1).wait_recv()
@@ -651,17 +676,16 @@
 
     lax.fori_loop(0, group, gradients_z, 0)
 
-
-    chunk = SUBLANES
 
     def point(index, acc):
         plane = lax.div(index, rows // chunk)
         at = pl.ds(pl.multiple_of(lax.rem(index, rows // chunk) * chunk, chunk), chunk)
         uz, uy, ux = grad_z[0, plane, at], grad_y[0, plane, at], grad_x[0, plane, at]
         dz, dy, dx = grad_z[1, plane, at], grad_y[1, plane, at], grad_x[1, plane, at]
-        energy, d_up, d_down, d_uu, d_ud, d_dd = xc_point(
+        energy, d_up, d_down, d_uu, d_ud, d_dd = xc_gradient(
             main[0, REACH + plane, at],
             main[1, REACH + plane, at],
+            [known[i, plane, at] for i in range(KNOWN)],
             uz * uz + uy * uy + ux * ux,
             uz * dz + uy * dy + ux * dx,
             dz * dz + dy * dy + dx * dx,
@@ -706,7 +730,6 @@
         flux_z_copy(1, me - group).start()
 
     energy_xc = jnp.sum(energy_acc) * (1.0 / cells)
-
     for spin in range(2):
         flux_out[:, spin] = jnp.where(
             sub_row < REACH, grad_y[spin, :, :SUBLANES], grad_y[spin, :, rows - SUBLANES :]
@@ -719,7 +742,6 @@
     @pl.when(left)
     def _():
         flux_y_copy(1, me - 1).start()
-
 
     @pl.when(me == first_device)
     def _():
@@ -739,15 +761,12 @@
 
         lax.fori_loop(0, planes_k, mix, 0)
 
-
     for spin in range(2):
         v_own[spin] = v_own[spin] - slope_x(grad_x[spin])
-
 
     loads[4].wait()
     others = pl.ds(0, devices - 1)
     remote(spec_out.at[others], spec_in.at[others], spec_s, spec_r, me).wait_recv()
-
     lane = lax.broadcasted_iota(jnp.int32, (1, 1, width_x), 2)
     first = lane == 0
     high, low = split(spec_in[...].reshape(depth * 2 * slots, width_x))
@@ -766,7 +785,6 @@
                     :, :, t * LANES : (t + 1) * LANES
                 ]
 
-
     n1, n2 = z_mid.shape[:2]
     full = n1 * n2
 
@@ -788,7 +806,6 @@
         return carry
 
     lax.fori_loop(0, 2 * tiles, fore, 0)
-
     lane = lax.broadcasted_iota(jnp.int32, (slots, LANES), 1)
 
     def back(col, carry):
@@ -818,7 +835,6 @@
         return carry
 
     lax.fori_loop(0, 2 * tiles, back, 0)
-
     for t in range(tiles):
         keep = lax.broadcasted_iota(jnp.int32, (1, 1, LANES), 2) + t * LANES == 0
         plus_re, plus_im = z_in[:, 0, t], z_in[:, 1, t]
@@ -832,17 +848,15 @@
     high, low = split(x_in[...].reshape(depth * 2 * slots, 2 * width_x))
     back_out[...] = jnp.concatenate(from_right(7, high, low), axis=1).reshape(back_out.shape)
 
-
     def back_copy(peer, slot):
         return remote(
             back_out.at[peer], back_in.at[slot], back_s, back_r, peer
         )
 
+    around(lambda peer: back_copy(peer, me).start(), last=crossing)
     around(lambda peer: back_copy(peer, me).start(), first=crossing)
-    around(lambda peer: back_copy(peer, me).start(), last=crossing)
     back_in[me] = back_out[me]
 
-
     @pl.when(left)
     def _():
         flux_y_copy(0, me).wait_recv()
@@ -858,7 +872,6 @@
     @pl.when(jnp.logical_not(right))
     def _():
         flux_in[1] = jnp.zeros(flux_in.shape[1:], jnp.float32)
-
 
     def divergence(plane, carry):
         for spin in range(2):
@@ -868,7 +881,6 @@
 
     lax.fori_loop(0, group, divergence, 0)
 
-
     @pl.when(exists_down)
     def _():
         flux_z_copy(0, me).wait_recv()
@@ -876,7 +888,6 @@
     @pl.when(exists_up)
     def _():
         flux_z_copy(1, me).wait_recv()
-
 
     def divergence_z(plane, carry):
         for spin in range(2):
@@ -884,7 +895,6 @@
         return carry
 
     lax.fori_loop(0, group, divergence_z, 0)
-
     def v_copy(b, peer, source):
         return remote(
             v_own.at[:, b], v_all.at[:, block(source)], v_s, v_r, peer
@@ -892,7 +902,6 @@
 
     in_group(lambda b, peer: v_copy(b, peer, member).start())
     v_all[:, block(member)] = v_own[:, member]
-
 
     acc = jnp.sum(spec_in[...] * back_out[...], axis=0)
     row = lax.broadcasted_iota(jnp.int32, acc.shape, 0)
@@ -909,14 +918,10 @@
 
 
     remote(back_out.at[others], back_in.at[others], back_s, back_r, me).wait_recv()
-
     high, low = split(back_in[...].reshape(depth * 2 * slots, width_x))
     hartree[...] = from_left(9, high, low)
-
     remote(v_own.at[:, mates], v_own.at[:, mates], v_s, v_r, me).wait_recv()
-
     remote(sums.at[others], sums.at[others], part_s, part_r, me).wait_recv()
-
 
     seven = main.at[:, mates]
     remote(seven, seven, main_s.at[0], main_r.at[0], me).wait_send()
@@ -1007,6 +1012,7 @@
         f32(tile_shape),
         f32(tile_shape),
         f32(tile_shape),
+        f32((KNOWN, group, rows, width_x)),
         f32(tall_shape),
         f32((group, 2, SUBLANES, width_x)),
         f32((2, group, 2, SUBLANES, width_x)),

time: 48.8 us -> 48 us (0.984)
  Pallas kernels: 48 us -> 47.2 us
    pallas_call x1, Pallas kernels: 47.1 us -> 46.3 us  [per_device(): pl.pallas_call(functools.partial(mega_kernel, devices, group, half, place...]
where the time goes in v4:
time: 48 us; the launch traced here: 47.8 us
  Pallas kernels  47.2 us (98%)
  between operations  0.64 us (1%)
    pallas_call x1, Pallas kernels, per_device(): pl.pallas_call(functools.partial(mega_kernel, devices, group, half, place...  46.3 us

profile of v4, /device:TPU:0, one launch (start us, length us, event | category | flops | bytes accessed | tf_op | source)
XLA Modules:
  0.0 47.8 jit_solution(3984963246101718584)
XLA Ops:
  0.6 46.3 %potential.1 = (f32[256,256]{1,0:T(8,128)S(1)}, f32[2,256,256]{2,1,0:T(8,128)S(1)}, f32[32,1,128]{2,1,0:T(1,128)S(1)}) custom-call(f32[2,256,256]{2,1,0:T(8,128)} %bitcast.4, f32[64,16,512]{2,1,0:T(8,128)} %refs_1_.1, bf16[4640,256]{1,0:T(8,128)(2,1)} %constant.2.clone.refs_2_), custom_call_target="tpu_custom_call" | custom-call | tf_op jit(solution)/shard_map/potential/pallas_call | solution.py:1042
  47.0 0.9 %join.1 = (f32[2,256,256]{2,1,0:T(8,128)}, f32[2]{0:T(128)}) custom-call(f32[256,256]{1,0:T(8,128)S(1)} %get-tuple-element.7.hartree, f32[2,256,256]{2,1,0:T(8,128)S(1)} %get-tuple-element.8.v_all, f32[32,1,128]{2,1,0:T(1,128)S(1)} %get-tuple-element.9.sums), custom_call_target="tpu_custom_call" | custom-call | tf_op jit(solution)/shard_map/join/pallas_call | solution.py:1057

commit v5 on v4

--- a/solution.py
+++ b/solution.py
@@ -502,12 +502,6 @@
     loads[1].wait()
     high, low = split(dens[0] + dens[1])
     spec_out[...] = from_left(0, high, low).reshape(spec_out.shape)
-    loads[2].wait()
-
-    @pl.when(me == edge_device)
-    def _():
-        edge_out[...] = khat[:, 0, :]
-        remote(edge_out, edge_in, edge_s, edge_r, first_device).start()
 
     def spec_copy(peer, slot):
         return remote(
@@ -533,6 +527,12 @@
         spec_copy(peer, me).start()
 
     around(start_spec, last=EARLY)
+    loads[2].wait()
+
+    @pl.when(me == edge_device)
+    def _():
+        edge_out[...] = khat[:, 0, :]
+        remote(edge_out, edge_in, edge_s, edge_r, first_device).start()
     main[:, REACH + member] = dens[:, block(member)]
     halo_in[member] = halo_out[member]
     spec_in[me] = spec_out[me]

time: 48 us -> 48.3 us (level)
  no operation moved by 1% of the time
where the time goes in v5:
time: 48.3 us; the launch traced here: 48.2 us
  Pallas kernels  47.6 us (99%)
  between operations  0.64 us (1%)
    pallas_call x1, Pallas kernels, per_device(): pl.pallas_call(functools.partial(mega_kernel, devices, group, half, place...  46.7 us

profile of v5, /device:TPU:0, one launch (start us, length us, event | category | flops | bytes accessed | tf_op | source)
XLA Modules:
  0.0 48.2 jit_solution(17834357238467743901)
XLA Ops:
  0.6 46.7 %potential.1 = (f32[256,256]{1,0:T(8,128)S(1)}, f32[2,256,256]{2,1,0:T(8,128)S(1)}, f32[32,1,128]{2,1,0:T(1,128)S(1)}) custom-call(f32[2,256,256]{2,1,0:T(8,128)} %bitcast.4, f32[64,16,512]{2,1,0:T(8,128)} %refs_1_.1, bf16[4640,256]{1,0:T(8,128)(2,1)} %constant.2.clone.refs_2_), custom_call_target="tpu_custom_call" | custom-call | tf_op jit(solution)/shard_map/potential/pallas_call | solution.py:1042
  47.3 0.9 %join.1 = (f32[2,256,256]{2,1,0:T(8,128)}, f32[2]{0:T(128)}) custom-call(f32[256,256]{1,0:T(8,128)S(1)} %get-tuple-element.7.hartree, f32[2,256,256]{2,1,0:T(8,128)S(1)} %get-tuple-element.8.v_all, f32[32,1,128]{2,1,0:T(1,128)S(1)} %get-tuple-element.9.sums), custom_call_target="tpu_custom_call" | custom-call | tf_op jit(solution)/shard_map/join/pallas_call | solution.py:1057
